TPU v7x, 256 devices: a whole 4x4x8 slice. The times are simulated.
256 devices in a mesh: tm: 16 (over z, y_hi), rows: 16 (over y_lo, x, core).
Axes of the slice: x: 4, y: 4 (y_hi: 2, y_lo: 2; y = y_hi * 2 + y_lo), z: 8, core: 2. Of those that a mesh axis runs over, the one named last changes fastest.
Arguments:
- upstream: bfloat16 [64, 128, 128, 128], P('tm', 'rows'), may hold values from -6 to 6
- saved_first: bfloat16 [64, 128, 128, 128], P('tm', 'rows'), may hold values from -8 to 8
- saved_second: bfloat16 [64, 128, 128, 128], P('tm', 'rows'), may hold values from -8 to 8
- weight_first: bfloat16 [3456, 128], replicated, may hold values from -0.109375 to 0.109375
- weight_second: bfloat16 [3456, 128], replicated, may hold values from -0.109375 to 0.109375
Outputs:
- grad_input: bfloat16 [64, 128, 128, 128], P('tm', 'rows')
- wgrad_first: float32 [3456, 128], P('tm')
- wgrad_second: float32 [3456, 128], P('tm')
All inputs are finite; a program needn't handle non-finite values.
Results may differ from a plain program's by a relative error of at most 0.005.
Values may be sent and summed in bfloat16 or wider, within the bound.
No kernel may reach another device: no remote copies, remote signals or barrier semaphores. Data moves between devices by JAX's collectives and lax.ppermute only.
A program may use at most 64 MiB of HBM per device.

v0:
```python
import math

import jax
import jax.numpy as jnp
from jax import lax
from jax.experimental import pallas as pl
from jax.experimental.pallas import tpu as pltpu
from jax.sharding import Mesh
from jax.sharding import PartitionSpec as P


TM = ("z", "yh")
PLANE = ("yh", "yl", "x")
ROWS = ("yl", "x", "core")
BF16 = jnp.bfloat16
F32 = jnp.float32
CH = 128


PAD = 32
ROW = 128


def local_call(kernel, outs, scratch, mebibytes, *args):
    scalar = pl.BlockSpec(memory_space=pltpu.SMEM)
    return pl.pallas_call(
        kernel,
        out_shape=outs,
        in_specs=[scalar if a.dtype == jnp.int32 else pl.BlockSpec() for a in args],
        scratch_shapes=scratch,
        compiler_params=pltpu.CompilerParams(vmem_limit_bytes=mebibytes * 1024 * 1024),
    )(*args)


def after(value, *others):
    return lax.optimization_barrier((value, *others))[0]


def store_shifted(dest, base, part):
    size = part.shape[0]
    wide = part.astype(F32)
    column = lax.broadcasted_iota(jnp.int32, (size, CH), 0) % 128
    later = jnp.where(column == 127, 0.0, pltpu.roll(wide, size - 1, 0))
    before = jnp.where(column == 0, 0.0, pltpu.roll(wide, 1, 0))
    dest[base : base + size, 0:CH] = later.astype(BF16)
    dest[base : base + size, CH : 2 * CH] = part
    dest[base : base + size, 2 * CH : 3 * CH] = before.astype(BF16)


def with_rows(above, own, below, frame, at, rows):
    size = rows * ROW
    return [
        (above, frame, 2 * ROW - size, size),
        (own, at, 0, own.shape[1]),
        (below, frame, 0, size),
    ]


def next_frame(edges, own, frame, rows):
    size = rows * ROW
    return [
        (edges, frame, 2 * ROW - size, size),
        (own, frame, 0, own.shape[1]),
        (edges, frame, 2 * ROW, size),
    ]


def whole(ref, frame):
    return [(ref, frame, 0, ref.shape[1])]


def store_frames(dest, frames, first=0):
    stride = sum(piece[3] for piece in frames[0])
    for frame, pieces in enumerate(frames):
        base = (first + frame) * stride
        for ref, at, begin, rows in pieces:
            step = min(rows, 256)
            for start in range(begin, begin + rows, step):
                store_shifted(dest, base, ref[at, start : start + step])
                base += step


def toeplitz_kernel(weight, out):
    zero = jnp.zeros((CH, CH), BF16)
    for tap in range(9):
        for p in range(3):
            at = (9 * p + tap) * CH
            turned = weight[at : at + CH, :].T
            for j in range(2):
                row = (9 * (j + 2 - p) + tap) * CH
                out[row : row + CH, j * CH : (j + 1) * CH] = turned
        out[(27 + tap) * CH : (28 + tap) * CH, 0:CH] = zero
        out[tap * CH : (tap + 1) * CH, CH : 2 * CH] = zero


def toeplitz(weight):
    return local_call(toeplitz_kernel, jax.ShapeDtypeStruct((36 * CH, 2 * CH), BF16), [], 16, weight)


def spread_two(wide, base, saved, first, taps, out, at_out):
    positions = out.shape[1]
    stride = positions + 2 * ROW
    block = positions // 2
    for at in range(0, positions, block):
        lhs = jnp.concatenate(
            [
                wide[start : start + block, :]
                for frame in range(4)
                for q in range(3)
                for start in [(base + frame) * stride + at + (2 - q) * ROW]
            ],
            axis=1,
        )
        spread = jnp.dot(lhs, taps[...], preferred_element_type=F32)
        for j in range(2):
            value = saved[first + j, at : at + block, :].astype(F32)
            sigma = jax.nn.sigmoid(value)
            slope = sigma * (1.0 + value * (1.0 - sigma))
            out[at_out + j, at : at + block, :] = (spread[:, j * CH : (j + 1) * CH] * slope).astype(BF16)


def spread_mid(above, own, below, saved, taps, band, bands, following):
    positions = saved.shape[1]
    first = 2 if following else 0

    def kernel(band, above, own, below, saved, taps, *rest):
        out, wide, near = rest[-3:]
        frames = [with_rows(above, own, below, f, f, 2) for f in range(first, 4)]
        if following:
            frames += [next_frame(rest[0], rest[1], f, 2) for f in range(2)]
        store_frames(wide, frames)
        for j in range(2):
            near[j, 0:ROW, :] = above[first + j, 2 * ROW : 3 * ROW, :]
            near[j, ROW : ROW + positions, :] = saved[first + j]
            near[j, ROW + positions :, :] = below[first + j, 2 * ROW : 3 * ROW, :]
        spread_two(wide, 0, near, 0, taps, out, 0)

        def clear(at):
            for j in range(2):
                out[j, at : at + ROW, :] = jnp.zeros((ROW, CH), BF16)

        pl.when(band[0] == 0)(lambda: clear(0))
        pl.when(band[0] == bands - 1)(lambda: clear(ROW + positions))

    extended = (2, positions + 2 * ROW, CH)
    return local_call(
        kernel,
        jax.ShapeDtypeStruct(extended, BF16),
        [pltpu.VMEM((4 * (positions + 4 * ROW), 3 * CH), BF16), pltpu.VMEM(extended, BF16)],
        12,
        band, above, own, below, saved, taps, *following,
    )


def spread_all(low, high, later, saved, taps):
    def kernel(low, high, later, saved, taps, out, wide):
        store_frames(wide, [whole(ref, f) for ref in (low, high, later) for f in range(2)])
        spread_two(wide, 0, saved, 0, taps, out, 0)
        spread_two(wide, 2, saved, 2, taps, out, 2)

    return local_call(
        kernel,
        jax.ShapeDtypeStruct(saved.shape, BF16),
        [pltpu.VMEM((6 * low.shape[1], 3 * CH), BF16)],
        16,
        low, high, later, saved, taps,
    )


def store_share(out, total):
    planes, depth = out.shape[0], out.shape[1] // PAD
    chips = planes // 2
    share = 27 * CH // (2 * depth)
    for z in range(depth):
        for plane in range(planes):
            block, chip = 2 * z + plane // chips, plane % chips
            values = []
            for row in range(chip * PAD, (chip + 1) * PAD, 8):
                if row < share:
                    tap, line = divmod(block * share + row, CH)
                    p, tap = divmod(tap, 9)
                    values.append(total[p * CH + line : p * CH + line + 8, tap * CH : (tap + 1) * CH])
                else:
                    values.append(jnp.zeros((8, CH), F32))
            out[plane, z * PAD : (z + 1) * PAD, :] = jnp.concatenate(values).astype(BF16)


def store_acts(turned, saved, frames):
    for at, frame in enumerate(frames):
        value = saved[frame].astype(F32)
        turned[at * CH : (at + 1) * CH, :] = (value * jax.nn.sigmoid(value)).astype(BF16).T


def add_products(total, turned, wide, frames, first_frame, first_act, acts):
    positions = turned.shape[1]
    stride = positions + 2 * ROW
    for at in range(frames):
        frame = first_frame + at
        lowest = max(0, first_act - (frame - 2))
        top = min(2, first_act + acts - 1 - (frame - 2))
        s = frame - 2 + lowest - first_act
        rhs = jnp.concatenate(
            [
                wide[start : start + positions, :]
                for q in range(3)
                for start in [at * stride + (2 - q) * ROW]
            ],
            axis=1,
        )
        lhs = turned[s * CH : (s + top - lowest + 1) * CH, :]
        total[lowest * CH : (top + 1) * CH, :] += jnp.dot(lhs, rhs, preferred_element_type=F32)


TOTAL = (3 * CH, 9 * CH)


def sums(above, up, below, edges, later, saved_second, low, high, saved_first, planes, depth):
    positions = saved_first.shape[1]
    stride = positions + 2 * ROW

    def kernel(above, up, below, edges, later, s2, low, high, s1, share, partial, wide, acts, acts_first, total):
        store_acts(acts, s2, range(4))
        store_frames(wide, [with_rows(above, up, below, f, f, 1) for f in range(4)])
        store_frames(wide, [next_frame(edges, later, f, 1) for f in range(2)], 4)
        total[...] = jnp.zeros(TOTAL, F32)
        add_products(total, acts, wide, 6, 0, 0, 4)
        store_share(share, total)
        store_acts(acts_first, s1, range(4))
        store_frames(wide, [whole(ref, f) for ref in (low, high) for f in range(2)])
        partial[...] = jnp.zeros(TOTAL, F32)
        add_products(partial, acts_first, wide, 4, 0, 0, 4)

    return local_call(
        kernel,
        (
            jax.ShapeDtypeStruct((planes, depth * PAD, CH), BF16),
            jax.ShapeDtypeStruct(TOTAL, F32),
        ),
        [
            pltpu.VMEM((6 * stride, 3 * CH), BF16),
            pltpu.VMEM((4 * CH, positions), BF16),
            pltpu.VMEM((4 * CH, positions), BF16),
            pltpu.VMEM(TOTAL, F32),
        ],
        16,
        above, up, below, edges, later, saved_second, low, high, saved_first,
    )


def kept_and_sent(core, partial, later, saved_first, second):
    positions = saved_first.shape[1]

    def kernel(core, partial, later, saved, second, kept, sent, wide, acts, total):
        store_acts(acts, saved, (2, 3))
        store_frames(wide, [whole(later, f) for f in range(2)])
        total[...] = partial[...]
        add_products(total, acts, wide, 2, 4, 2, 2)

        def store(first_to, second_to):
            store_share(first_to, total)
            second_to[...] = second[...]

        pl.when(core[0] == 0)(lambda: store(kept, sent))
        pl.when(core[0] == 1)(lambda: store(sent, kept))

    out = jax.ShapeDtypeStruct(second.shape, BF16)
    return local_call(
        kernel,
        (out, out),
        [
            pltpu.VMEM((2 * later.shape[1], 3 * CH), BF16),
            pltpu.VMEM((2 * CH, positions), BF16),
            pltpu.VMEM(TOTAL, F32),
        ],
        12,
        core, partial, later, saved_first, second,
    )


def moved(block, axis, step):
    count = lax.axis_size(axis)
    route = [(i, i + step) for i in range(count) if 0 <= i + step < count]
    return lax.ppermute(block, axis, route)


def exchanged(pieces, axis):
    return lax.all_to_all(pieces, axis, split_axis=0, concat_axis=0, tiled=True)


def body(upstream, saved_first, saved_second, weight_first, weight_second):
    frames, height, width, chans = upstream.shape
    planes, depth = lax.axis_size(PLANE), lax.axis_size("z")
    flat = lambda a: a.reshape(frames, height * width, chans)
    up, s1, s2 = flat(upstream), flat(saved_first), flat(saved_second)

    band = lax.axis_index(ROWS).reshape(1)
    bands = lax.axis_size(ROWS)
    core = lax.axis_index("core").reshape(1)

    later = moved(up[:2], TM, -1)
    above = moved(jnp.concatenate([up[:, -2 * ROW :], s2[:, -ROW:]], axis=1), ROWS, 1)
    below = moved(jnp.concatenate([up[:, : 2 * ROW], s2[:, :ROW]], axis=1), ROWS, -1)
    edges = moved(jnp.concatenate([above[:2, : 2 * ROW], below[:2, : 2 * ROW]], axis=1), TM, -1)
    taps_second = toeplitz(weight_second)
    low = spread_mid(above, up, below, s2, taps_second, band, bands, ())
    mid_later = moved(low, TM, -1)
    taps_first = toeplitz(after(weight_first, low))
    high = spread_mid(
        above, up, below, after(s2, taps_first), taps_second, band, bands, (edges, later)
    )
    second, partial = sums(above, up, below, edges, later, s2, low, high, s1, planes, depth)
    kept, sent = kept_and_sent(core, partial, mid_later, s1, second)
    received = lax.ppermute(sent, "core", [(0, 1), (1, 0)])
    half = (kept.astype(F32) + received.astype(F32)).astype(BF16)
    part = exchanged(half, PLANE)
    part = part.astype(F32).sum(axis=0).astype(BF16)
    grad_input = spread_all(low, high, mid_later, s1, taps_first)
    part = exchanged(part.reshape(depth, PAD, CH), "z").astype(F32).sum(axis=0)
    factor = 1.0 / math.sqrt(
        frames * lax.axis_size(TM) * height * lax.axis_size(ROWS) * width
    )
    every = exchanged(jnp.broadcast_to(part * factor, (lax.axis_size(ROWS), PAD, CH)), ROWS)
    every = every.reshape(-1, 2, PAD, CH)
    share = weight_first.shape[0] // lax.axis_size(TM)
    share_first, share_second = (every[:, c].reshape(-1, CH)[:share] for c in range(2))
    return (grad_input.reshape(upstream.shape), share_first, share_second)


def solution(mesh):
    finer = Mesh(mesh.devices.reshape(8, 2, 2, 4, 2), ("z", "yh", "yl", "x", "core"))
    field = P(TM, ROWS, None, None)
    in_specs = (field, field, field, P(), P())
    out_specs = (field, P(TM, None), P(TM, None))
    return jax.shard_map(body, mesh=finer, in_specs=in_specs, out_specs=out_specs, check_vma=False)
```

profile of v0, /device:TPU:1, one launch (start us, length us, event | category | flops | bytes accessed | tf_op | source)
XLA Modules:
  0.0 140.3 jit_solution(15559123798990494802)
XLA Ops:
  3.5 4.6 %collective-permute-start = (bf16[4,384,128]{2,1,0:T(8,128)(2,1)}, bf16[4,384,128]{2,1,0:T(8,128)(2,1)}, u32[]{:S(2)}, u32[]{:S(2)}) collective-permute-start(bf16[4,384,128]{2,1,0:T(8,128)(2,1)} %pad_maximum_fusion), channel_id=1, source_target_pairs={{0,1},{1,2},{2,3},{3,4},{4,5},{5,6},{6,7},{7,8},{8,9},{9,10},{10,1... | collective-permute-start | bytes 1179656 | tf_op jit(solution)/shard_map/ppermute | solution.py:283
  8.9 2.6 %collective-permute-start.1 = (bf16[4,384,128]{2,1,0:T(8,128)(2,1)}, bf16[4,384,128]{2,1,0:T(8,128)(2,1)}, u32[]{:S(2)}, u32[]{:S(2)}) collective-permute-start(bf16[4,384,128]{2,1,0:T(8,128)(2,1)} %pad_maximum_fusion.1), channel_id=1, source_target_pairs={{1,0},{2,1},{3,2},{4,3},{5,4},{6,5},{7,6},{8,7},{9,8},{10,9},{11,1... | collective-permute-start | bytes 1179656 | tf_op jit(solution)/shard_map/ppermute | solution.py:283
  11.6 1.2 copy-done.13
  13.1 5.2 %collective-permute-done.1.below = bf16[4,384,128]{2,1,0:T(8,128)(2,1)} collective-permute-done((bf16[4,384,128]{2,1,0:T(8,128)(2,1)}, bf16[4,384,128]{2,1,0:T(8,128)(2,1)}, u32[]{:S(2)}, u32[]{:S(2)}) %collective-permute-start.1) | collective-permute-done | bytes 393248 | tf_op jit(solution)/shard_map/ppermute | solution.py:283
  18.3 1.2 copy-done.1
  19.5 4.6 %shard_map.77.low = bf16[2,1280,128]{2,1,0:T(8,128)(2,1)S(1)} custom-call(s32[1]{0:T(128)} %bitcast.band, bf16[4,384,128]{2,1,0:T(8,128)(2,1)} %collective-permute-done.above, bf16[4,1024,128]{2,1,0:T(8,128)(2,1)S(1)} %bitcast.12, bf16[4,384,128]{2,1,0:T(8,128)(2,1)} %collective-permute-done.1.below, bf16[4,1024,128]{2,1,0:T(8,128)(2,1)S(1)} %bitcast.16, ...), custom_call_target="tpu_custom_call" | custom-call | tf_op jit(solution)/shard_map/pallas_call | solution.py:26
  24.1 1.4 %collective-permute-start.4 = (bf16[2,1280,128]{2,1,0:T(8,128)(2,1)S(1)}, bf16[2,1280,128]{2,1,0:T(8,128)(2,1)S(1)}, u32[]{:S(2)}, u32[]{:S(2)}) collective-permute-start(bf16[2,1280,128]{2,1,0:T(8,128)(2,1)S(1)} %shard_map.77.low), channel_id=1, source_target_pairs={{16,0},{32,16},{48,32},{64,48},{80,64},{96,80},{112,96},{128,112},... | collective-permute-start | bytes 1966088 | tf_op jit(solution)/shard_map/ppermute | solution.py:283
  25.6 1.4 %collective-permute-start.3 = (bf16[2,1024,128]{2,1,0:T(8,128)(2,1)S(1)}, bf16[2,1024,128]{2,1,0:T(8,128)(2,1)S(1)}, u32[]{:S(2)}, u32[]{:S(2)}) collective-permute-start(bf16[2,1024,128]{2,1,0:T(8,128)(2,1)S(1)} %bitcast.23), channel_id=1, source_target_pairs={{16,0},{32,16},{48,32},{64,48},{80,64},{96,80},{112,96},{128,112},... | collective-permute-start | bytes 1572872 | tf_op jit(solution)/shard_map/ppermute | solution.py:283
  28.9 1.3 collective-permute-start.2
  30.6 1.4 %copy-done.3 = bf16[4608,256]{1,0:T(8,128)(2,1)} copy-done((bf16[4608,256]{1,0:T(8,128)(2,1)}, bf16[4608,256]{1,0:T(8,128)(2,1)S(1)}, u32[]{:S(2)}) %copy-start.3) | copy-done | bytes 2359320
  32.0 21.9 %collective-permute-done.3.rest_1_.later = bf16[2,1024,128]{2,1,0:T(8,128)(2,1)S(1)} collective-permute-done((bf16[2,1024,128]{2,1,0:T(8,128)(2,1)S(1)}, bf16[2,1024,128]{2,1,0:T(8,128)(2,1)S(1)}, u32[]{:S(2)}, u32[]{:S(2)}) %collective-permute-start.3) | collective-permute-done | bytes 524320 | tf_op jit(solution)/shard_map/ppermute | solution.py:283
  53.9 2.8 %collective-permute-done.2.rest_0_.edges = bf16[2,512,128]{2,1,0:T(8,128)(2,1)S(1)} collective-permute-done((bf16[2,512,128]{2,1,0:T(8,128)(2,1)S(1)}, bf16[2,512,128]{2,1,0:T(8,128)(2,1)S(1)}, u32[]{:S(2)}, u32[]{:S(2)}) %collective-permute-start.2) | collective-permute-done | bytes 262176 | tf_op jit(solution)/shard_map/ppermute | solution.py:283
  56.7 4.7 %shard_map.79.high = bf16[2,1280,128]{2,1,0:T(8,128)(2,1)S(1)} custom-call(s32[1]{0:T(128)} %bitcast.band, bf16[4,384,128]{2,1,0:T(8,128)(2,1)} %collective-permute-done.above, bf16[4,1024,128]{2,1,0:T(8,128)(2,1)S(1)} %bitcast.13, bf16[4,384,128]{2,1,0:T(8,128)(2,1)} %collective-permute-done.1.below, bf16[4,1024,128]{2,1,0:T(8,128)(2,1)S(1)} %bitcast.17, ...), custom_call_target="tpu_custom_call" | custom-call | tf_op jit(solution)/shard_map/pallas_call | solution.py:26
  61.5 10.1 %shard_map.81 = (bf16[16,256,128]{2,1,0:T(8,128)(2,1)S(1)}, f32[384,1152]{1,0:T(8,128)S(1)}) custom-call(bf16[4,384,128]{2,1,0:T(8,128)(2,1)} %collective-permute-done.above, bf16[4,1024,128]{2,1,0:T(8,128)(2,1)S(1)} %bitcast.14, bf16[4,384,128]{2,1,0:T(8,128)(2,1)} %collective-permute-done.1.below, ...), custom_call_target="tpu_custom_call" | custom-call | tf_op jit(solution)/shard_map/pallas_call | solution.py:26
  71.6 1.6 %shard_map.82 = (bf16[16,256,128]{2,1,0:T(8,128)(2,1)S(1)}, bf16[16,256,128]{2,1,0:T(8,128)(2,1)S(1)}) custom-call(s32[1]{0:T(128)} %bitcast.6.core, f32[384,1152]{1,0:T(8,128)S(1)} %get-tuple-element.11.partial, bf16[2,1280,128]{2,1,0:T(8,128)(2,1)S(1)} %collective-permute-done.4.later, bf16[4,1024,128]{2,1,0:T(8,128)(2,1)S(1)} %bitcast.20, ...), custom_call_target="tpu_custom_call" | custom-call | tf_op jit(solution)/shard_map/pallas_call | solution.py:26
  73.4 2.6 %collective-permute-done.5 = bf16[16,256,128]{2,1,0:T(8,128)(2,1)S(1)} collective-permute-done((bf16[16,256,128]{2,1,0:T(8,128)(2,1)S(1)}, bf16[16,256,128]{2,1,0:T(8,128)(2,1)S(1)}, u32[]{:S(2)}, u32[]{:S(2)}) %collective-permute-start.5) | collective-permute-done | bytes 1048608 | tf_op jit(solution)/shard_map/ppermute | solution.py:313
  76.3 27.7 %all_to_all.15 = bf16[16,256,128]{2,1,0:T(8,128)(2,1)} all-to-all(bf16[16,256,128]{2,1,0:T(8,128)(2,1)S(1)} %add_convert_fusion), channel_id=1, replica_groups=mesh['z'=8,'yh'=2,'yl'=2,'x'=4,'core'=2] {'yh','yl','x'}, dimensions={0} | all-to-all | bytes 2097152 | tf_op jit(solution)/shard_map/all_to_all | solution.py:287
  104.1 1.4 reduce_sum.21
  105.4 15.4 %all_to_all.16 = bf16[8,32,128]{2,1,0:T(8,128)(2,1)S(1)} all-to-all(bf16[8,32,128]{2,1,0:T(8,128)(2,1)S(1)} %bitcast.26), channel_id=1, replica_groups=mesh['z'=8,'yh'=2,'yl'=2,'x'=4,'core'=2] {'z'}, dimensions={0} | all-to-all | bytes 131072 | tf_op jit(solution)/shard_map/all_to_all | solution.py:287
  121.6 6.8 %all-to-all-start.2 = ((f32[16,32,128]{2,1,0:T(8,128)}), f32[16,32,128]{2,1,0:T(8,128)}, u32[]{:S(2)}, u32[]{:S(2)}) async-start(f32[16,32,128]{2,1,0:T(8,128)} %broadcast_in_dim.3), calls=%async_computation.2 | async-start | bytes 524288 | tf_op jit(solution)/shard_map/all_to_all | solution.py:287
  128.4 1.1 copy-done.8
  129.5 1.1 copy-done.10
  130.6 1.1 copy-done.12
  131.7 6.3 %shard_map.80 = bf16[4,1024,128]{2,1,0:T(8,128)(2,1)} custom-call(bf16[2,1280,128]{2,1,0:T(8,128)(2,1)S(1)} %copy-done.8, bf16[2,1280,128]{2,1,0:T(8,128)(2,1)S(1)} %copy-done.10, bf16[2,1280,128]{2,1,0:T(8,128)(2,1)S(1)} %copy-done.12, bf16[4,1024,128]{2,1,0:T(8,128)(2,1)S(1)} %bitcast.21, bf16[4608,256]{1,0:T(8,128)(2,1)S(1)} %copy-done.4), custom_call_target="tpu_custom_call" | custom-call | tf_op jit(solution)/shard_map/pallas_call | solution.py:26
  (45 shorter events, 9.7 us)
Async XLA Ops:
  3.5 14.8 %copy-start = (bf16[4,8,128,128]{3,2,1,0:T(8,128)(2,1)S(1)}, bf16[4,8,128,128]{3,2,1,0:T(8,128)(2,1)}, u32[]{:S(2)}) copy-start(bf16[4,8,128,128]{3,2,1,0:T(8,128)(2,1)} %param.5) | copy-start | bytes 3145732
  3.5 9.6 %collective-permute-start = (bf16[4,384,128]{2,1,0:T(8,128)(2,1)}, bf16[4,384,128]{2,1,0:T(8,128)(2,1)}, u32[]{:S(2)}, u32[]{:S(2)}) collective-permute-start(bf16[4,384,128]{2,1,0:T(8,128)(2,1)} %pad_maximum_fusion), channel_id=1, source_target_pairs={{0,1},{1,2},{2,3},{3,4},{4,5},{5,6},{6,7},{7,8},{8,9},{9,10},{10,1... | collective-permute-start | bytes 1179656 | tf_op jit(solution)/shard_map/ppermute | solution.py:283
  8.9 9.4 %collective-permute-start.1 = (bf16[4,384,128]{2,1,0:T(8,128)(2,1)}, bf16[4,384,128]{2,1,0:T(8,128)(2,1)}, u32[]{:S(2)}, u32[]{:S(2)}) collective-permute-start(bf16[4,384,128]{2,1,0:T(8,128)(2,1)} %pad_maximum_fusion.1), channel_id=1, source_target_pairs={{1,0},{2,1},{3,2},{4,3},{5,4},{6,5},{7,6},{8,7},{9,8},{10,9},{11,1... | collective-permute-start | bytes 1179656 | tf_op jit(solution)/shard_map/ppermute | solution.py:283
  11.5 1.2 copy-start.13
  18.3 1.2 copy-start.1
  24.1 37.4 %copy-start.7 = (bf16[2,1280,128]{2,1,0:T(8,128)(2,1)}, bf16[2,1280,128]{2,1,0:T(8,128)(2,1)S(1)}, u32[]{:S(2)}) copy-start(bf16[2,1280,128]{2,1,0:T(8,128)(2,1)S(1)} %shard_map.77.low) | copy-start | bytes 1966084
  24.1 6.1 %copy-start.14 = (bf16[3456,128]{1,0:T(8,128)(2,1)S(1)}, bf16[3456,128]{1,0:T(8,128)(2,1)}, u32[]{:S(2)}) copy-start(bf16[3456,128]{1,0:T(8,128)(2,1)} %weight.2) | copy-start | bytes 2654212
  24.1 47.5 %collective-permute-start.4 = (bf16[2,1280,128]{2,1,0:T(8,128)(2,1)S(1)}, bf16[2,1280,128]{2,1,0:T(8,128)(2,1)S(1)}, u32[]{:S(2)}, u32[]{:S(2)}) collective-permute-start(bf16[2,1280,128]{2,1,0:T(8,128)(2,1)S(1)} %shard_map.77.low), channel_id=1, source_target_pairs={{16,0},{32,16},{48,32},{64,48},{80,64},{96,80},{112,96},{128,112},... | collective-permute-start | bytes 1966088 | tf_op jit(solution)/shard_map/ppermute | solution.py:283
  25.6 31.1 %copy-start.2 = (bf16[4,8,128,128]{3,2,1,0:T(8,128)(2,1)S(1)}, bf16[4,8,128,128]{3,2,1,0:T(8,128)(2,1)}, u32[]{:S(2)}) copy-start(bf16[4,8,128,128]{3,2,1,0:T(8,128)(2,1)} %param.7) | copy-start | bytes 3145732
  25.6 28.3 %collective-permute-start.3 = (bf16[2,1024,128]{2,1,0:T(8,128)(2,1)S(1)}, bf16[2,1024,128]{2,1,0:T(8,128)(2,1)S(1)}, u32[]{:S(2)}, u32[]{:S(2)}) collective-permute-start(bf16[2,1024,128]{2,1,0:T(8,128)(2,1)S(1)} %bitcast.23), channel_id=1, source_target_pairs={{16,0},{32,16},{48,32},{64,48},{80,64},{96,80},{112,96},{128,112},... | collective-permute-start | bytes 1572872 | tf_op jit(solution)/shard_map/ppermute | solution.py:283
  28.9 27.8 %collective-permute-start.2 = (bf16[2,512,128]{2,1,0:T(8,128)(2,1)S(1)}, bf16[2,512,128]{2,1,0:T(8,128)(2,1)S(1)}, u32[]{:S(2)}, u32[]{:S(2)}) collective-permute-start(bf16[2,512,128]{2,1,0:T(8,128)(2,1)S(1)} %pad_maximum_fusion.2), channel_id=1, source_target_pairs={{16,0},{32,16},{48,32},{64,48},{80,64},{96,80},{112,96},{128,112},... | collective-permute-start | bytes 786440 | tf_op jit(solution)/shard_map/ppermute | solution.py:283
  30.6 1.4 %copy-start.3 = (bf16[4608,256]{1,0:T(8,128)(2,1)}, bf16[4608,256]{1,0:T(8,128)(2,1)S(1)}, u32[]{:S(2)}) copy-start(bf16[4608,256]{1,0:T(8,128)(2,1)S(1)} %shard_map.78.taps) | copy-start | bytes 7077892
  32.0 29.4 %copy-start.5 = (bf16[4,8,128,128]{3,2,1,0:T(8,128)(2,1)S(1)}, bf16[4,8,128,128]{3,2,1,0:T(8,128)(2,1)}, u32[]{:S(2)}) copy-start(bf16[4,8,128,128]{3,2,1,0:T(8,128)(2,1)} %param.6) | copy-start | bytes 3145732
  61.4 10.2 %copy-start.9 = (bf16[2,1280,128]{2,1,0:T(8,128)(2,1)}, bf16[2,1280,128]{2,1,0:T(8,128)(2,1)S(1)}, u32[]{:S(2)}) copy-start(bf16[2,1280,128]{2,1,0:T(8,128)(2,1)S(1)} %shard_map.79.high) | copy-start | bytes 1966084
  71.6 1.6 %copy-start.11 = (bf16[2,1280,128]{2,1,0:T(8,128)(2,1)}, bf16[2,1280,128]{2,1,0:T(8,128)(2,1)S(1)}, u32[]{:S(2)}) copy-start(bf16[2,1280,128]{2,1,0:T(8,128)(2,1)S(1)} %collective-permute-done.4.later) | copy-start | bytes 1966084
  73.3 2.7 %collective-permute-start.5 = (bf16[16,256,128]{2,1,0:T(8,128)(2,1)S(1)}, bf16[16,256,128]{2,1,0:T(8,128)(2,1)S(1)}, u32[]{:S(2)}, u32[]{:S(2)}) collective-permute-start(bf16[16,256,128]{2,1,0:T(8,128)(2,1)S(1)} %get-tuple-element.14), channel_id=1, source_target_pairs={{0,1},{1,0},{2,3},{3,2},{4,5},{5,4},{6,7},{7,6},{8,9},{9,8},{10,11... | collective-permute-start | bytes 3145736 | tf_op jit(solution)/shard_map/ppermute | solution.py:313
  76.3 52.1 %copy-start.4 = (bf16[4608,256]{1,0:T(8,128)(2,1)S(1)}, bf16[4608,256]{1,0:T(8,128)(2,1)}, u32[]{:S(2)}) copy-start(bf16[4608,256]{1,0:T(8,128)(2,1)} %copy-done.3) | copy-start | bytes 7077892
  76.3 52.1 %copy-start.6 = (bf16[4,8,128,128]{3,2,1,0:T(8,128)(2,1)S(1)}, bf16[4,8,128,128]{3,2,1,0:T(8,128)(2,1)}, u32[]{:S(2)}) copy-start(bf16[4,8,128,128]{3,2,1,0:T(8,128)(2,1)} %param.6) | copy-start | bytes 3145732
  121.6 16.4 %all-to-all-start.2 = ((f32[16,32,128]{2,1,0:T(8,128)}), f32[16,32,128]{2,1,0:T(8,128)}, u32[]{:S(2)}, u32[]{:S(2)}) async-start(f32[16,32,128]{2,1,0:T(8,128)} %broadcast_in_dim.3), calls=%async_computation.2 | async-start | bytes 524288 | tf_op jit(solution)/shard_map/all_to_all | solution.py:287
  128.4 1.1 copy-start.8
  129.5 1.1 copy-start.10
  130.6 1.1 copy-start.12
where the time goes:
time: 141 us; the launch traced here: 140 us
  blocking collectives  43.1 us (31%)
  waiting for transfers between devices  32.5 us (23%)
  Pallas kernels  28 us (20%)
  starting transfers between devices  18.3 us (13%)
  local copies, waits for them, and re-layouts  14.1 us (10%)
  other arithmetic  3.24 us (2%)
    all_to_all x2, blocking collectives, exchanged(): return lax.all_to_all(pieces, axis, split_axis=0, concat_axis=0, tiled=True)  43.1 us
    ppermute x5, waiting for transfers between devices, moved(): return lax.ppermute(block, axis, route)  29.9 us
    pallas_call x7, Pallas kernels, local_call(): pl.pallas_call(kernel, out_shape=outs, in_specs=[scalar if a.dtype == jnp...  28 us
    ppermute x5, starting transfers between devices, moved(): return lax.ppermute(block, axis, route)  11.4 us
    unnamed x30, local copies, waits for them, and re-layouts  7.13 us
    all_to_all x1, starting transfers between devices, exchanged(): return lax.all_to_all(pieces, axis, split_axis=0, concat_axis=0, tiled=True)  6.84 us
  transfers between devices with their start and end apart: 7, of which 4 were waited for; matrix products, arithmetic and copies ran while one was open for 2% of the time, Pallas kernels for 16%

commit v1 on v0

--- a/solution.py
+++ b/solution.py
@@ -18,22 +18,76 @@
 
 
 PAD = 32
+BLOCK = 512
 ROW = 128
 
 
-def local_call(kernel, outs, scratch, mebibytes, *args):
-    scalar = pl.BlockSpec(memory_space=pltpu.SMEM)
+def local_call(kernel, outs, scratch, mebibytes, *args, placed=()):
+    specs = [pl.BlockSpec(memory_space=pl.ANY) if at in placed else pl.BlockSpec() for at in range(len(args))]
     return pl.pallas_call(
         kernel,
         out_shape=outs,
-        in_specs=[scalar if a.dtype == jnp.int32 else pl.BlockSpec() for a in args],
+        in_specs=specs,
         scratch_shapes=scratch,
         compiler_params=pltpu.CompilerParams(vmem_limit_bytes=mebibytes * 1024 * 1024),
     )(*args)
 
 
-def after(value, *others):
-    return lax.optimization_barrier((value, *others))[0]
+def copied(parts, shapes, sources, space):
+    def kernel(*refs):
+        outs, sems = refs[len(sources) : -1], refs[-1]
+        copies = [
+            pltpu.make_async_copy(refs[source].at[at], outs[out].at[to], sems.at[n])
+            for n, (out, to, source, at) in enumerate(parts)
+        ]
+        for copy in copies:
+            copy.start()
+        for copy in copies:
+            copy.wait()
+
+    return pl.pallas_call(
+        kernel,
+        out_shape=[jax.ShapeDtypeStruct(shape, sources[0].dtype) for shape in shapes],
+        in_specs=[pl.BlockSpec(memory_space=space)] * len(sources),
+        scratch_shapes=[pltpu.SemaphoreType.DMA((len(parts),))],
+        compiler_params=pltpu.CompilerParams(vmem_limit_bytes=8 * 1024 * 1024),
+    )(*sources)
+
+
+def rows_of(frames, begin, size):
+    return (slice(0, frames), slice(begin, begin + size))
+
+
+def added(own, other):
+    def kernel(own, other, out):
+        for at in range(out.shape[0]):
+            out[at] = (own[at].astype(F32) + other[at].astype(F32)).astype(BF16)
+
+    return local_call(kernel, jax.ShapeDtypeStruct(own.shape, BF16), [], 8, own, other)
+
+
+def summed_copies(pieces, copies, factor):
+    def kernel(pieces, out):
+        total = pieces[0].astype(F32)
+        for at in range(1, pieces.shape[0]):
+            total += pieces[at].astype(F32)
+        for at in range(copies):
+            out[at] = total * factor
+
+    out = jax.ShapeDtypeStruct((copies, *pieces.shape[1:]), F32)
+    return local_call(kernel, out, [], 8, pieces)
+
+
+def shares(every, share):
+    def kernel(every, first, second):
+        for out, core in ((first, 0), (second, 1)):
+            for chip in range(every.shape[0] // 2):
+                rows = min(PAD, share - chip * PAD)
+                if rows > 0:
+                    out[chip * PAD : chip * PAD + rows, :] = every[2 * chip + core, 0:rows, :]
+
+    out = jax.ShapeDtypeStruct((share, CH), F32)
+    return local_call(kernel, (out, out), [], 8, every)
 
 
 def store_shifted(dest, base, part):
@@ -100,8 +154,8 @@
 def spread_two(wide, base, saved, first, taps, out, at_out):
     positions = out.shape[1]
     stride = positions + 2 * ROW
-    block = positions // 2
-    for at in range(0, positions, block):
+    for at in range(0, positions, BLOCK):
+        block = min(BLOCK, positions - at)
         lhs = jnp.concatenate(
             [
                 wide[start : start + block, :]
@@ -119,41 +173,51 @@
             out[at_out + j, at : at + block, :] = (spread[:, j * CH : (j + 1) * CH] * slope).astype(BF16)
 
 
-def spread_mid(above, own, below, saved, taps, band, bands, following):
+def spread_mid(above, own, below, saved, taps, bands, following):
     positions = saved.shape[1]
     first = 2 if following else 0
 
-    def kernel(band, above, own, below, saved, taps, *rest):
-        out, wide, near = rest[-3:]
+    def kernel(above, own, below, saved, taps, *rest):
+        out, wide, near, sem = rest[-4:]
+        inner = near.at[:, ROW : ROW + positions, :]
+        copy = pltpu.make_async_copy(saved.at[first : first + 2], inner, sem)
+        copy.start()
         frames = [with_rows(above, own, below, f, f, 2) for f in range(first, 4)]
         if following:
             frames += [next_frame(rest[0], rest[1], f, 2) for f in range(2)]
         store_frames(wide, frames)
         for j in range(2):
             near[j, 0:ROW, :] = above[first + j, 2 * ROW : 3 * ROW, :]
-            near[j, ROW : ROW + positions, :] = saved[first + j]
             near[j, ROW + positions :, :] = below[first + j, 2 * ROW : 3 * ROW, :]
+        copy.wait()
         spread_two(wide, 0, near, 0, taps, out, 0)
 
         def clear(at):
             for j in range(2):
                 out[j, at : at + ROW, :] = jnp.zeros((ROW, CH), BF16)
 
-        pl.when(band[0] == 0)(lambda: clear(0))
-        pl.when(band[0] == bands - 1)(lambda: clear(ROW + positions))
+        band = lax.axis_index(ROWS)
+        pl.when(band == 0)(lambda: clear(0))
+        pl.when(band == bands - 1)(lambda: clear(ROW + positions))
 
     extended = (2, positions + 2 * ROW, CH)
     return local_call(
         kernel,
         jax.ShapeDtypeStruct(extended, BF16),
-        [pltpu.VMEM((4 * (positions + 4 * ROW), 3 * CH), BF16), pltpu.VMEM(extended, BF16)],
+        [
+            pltpu.VMEM((4 * (positions + 4 * ROW), 3 * CH), BF16),
+            pltpu.VMEM(extended, BF16),
+            pltpu.SemaphoreType.DMA,
+        ],
         12,
-        band, above, own, below, saved, taps, *following,
-    )
-
-
-def spread_all(low, high, later, saved, taps):
-    def kernel(low, high, later, saved, taps, out, wide):
+        above, own, below, saved, taps, *following,
+        placed=(3,),
+    )
+
+
+def spread_all(low, high, later, saved, weight):
+    def kernel(low, high, later, saved, weight, out, wide, taps):
+        toeplitz_kernel(weight, taps)
         store_frames(wide, [whole(ref, f) for ref in (low, high, later) for f in range(2)])
         spread_two(wide, 0, saved, 0, taps, out, 0)
         spread_two(wide, 2, saved, 2, taps, out, 2)
@@ -161,9 +225,9 @@
     return local_call(
         kernel,
         jax.ShapeDtypeStruct(saved.shape, BF16),
-        [pltpu.VMEM((6 * low.shape[1], 3 * CH), BF16)],
-        16,
-        low, high, later, saved, taps,
+        [pltpu.VMEM((6 * low.shape[1], 3 * CH), BF16), pltpu.VMEM((36 * CH, 2 * CH), BF16)],
+        18,
+        low, high, later, saved, weight,
     )
 
 
@@ -247,10 +311,10 @@
     )
 
 
-def kept_and_sent(core, partial, later, saved_first, second):
+def kept_and_sent(partial, later, saved_first, second):
     positions = saved_first.shape[1]
 
-    def kernel(core, partial, later, saved, second, kept, sent, wide, acts, total):
+    def kernel(partial, later, saved, second, kept, sent, wide, acts, total):
         store_acts(acts, saved, (2, 3))
         store_frames(wide, [whole(later, f) for f in range(2)])
         total[...] = partial[...]
@@ -260,8 +324,9 @@
             store_share(first_to, total)
             second_to[...] = second[...]
 
-        pl.when(core[0] == 0)(lambda: store(kept, sent))
-        pl.when(core[0] == 1)(lambda: store(sent, kept))
+        core = lax.axis_index("core")
+        pl.when(core == 0)(lambda: store(kept, sent))
+        pl.when(core == 1)(lambda: store(sent, kept))
 
     out = jax.ShapeDtypeStruct(second.shape, BF16)
     return local_call(
@@ -273,7 +338,7 @@
             pltpu.VMEM(TOTAL, F32),
         ],
         12,
-        core, partial, later, saved_first, second,
+        partial, later, saved_first, second,
     )
 
 
@@ -293,36 +358,53 @@
     flat = lambda a: a.reshape(frames, height * width, chans)
     up, s1, s2 = flat(upstream), flat(saved_first), flat(saved_second)
 
-    band = lax.axis_index(ROWS).reshape(1)
     bands = lax.axis_size(ROWS)
-    core = lax.axis_index("core").reshape(1)
-
-    later = moved(up[:2], TM, -1)
-    above = moved(jnp.concatenate([up[:, -2 * ROW :], s2[:, -ROW:]], axis=1), ROWS, 1)
-    below = moved(jnp.concatenate([up[:, : 2 * ROW], s2[:, :ROW]], axis=1), ROWS, -1)
-    edges = moved(jnp.concatenate([above[:2, : 2 * ROW], below[:2, : 2 * ROW]], axis=1), TM, -1)
+
+    size = up.shape[1]
+    tail, head, start, up_near, s2_near = copied(
+        (
+            (0, rows_of(4, 0, 2 * ROW), 0, rows_of(4, size - 2 * ROW, 2 * ROW)),
+            (0, rows_of(4, 2 * ROW, ROW), 1, rows_of(4, size - ROW, ROW)),
+            (1, rows_of(4, 0, 2 * ROW), 0, rows_of(4, 0, 2 * ROW)),
+            (1, rows_of(4, 2 * ROW, ROW), 1, rows_of(4, 0, ROW)),
+            (2, rows_of(2, 0, size), 0, rows_of(2, 0, size)),
+            (3, rows_of(4, 0, size), 0, rows_of(4, 0, size)),
+            (4, rows_of(4, 0, size), 1, rows_of(4, 0, size)),
+        ),
+        ((frames, 3 * ROW, CH), (frames, 3 * ROW, CH), (2, size, CH), up.shape, up.shape),
+        tuple(pltpu.with_memory_space_constraint(a, pltpu.HBM) for a in (up, s2)),
+        pltpu.HBM,
+    )
+    above = moved(tail, ROWS, 1)
+    below = moved(head, ROWS, -1)
+    later = moved(start, TM, -1)
+    (packed,) = copied(
+        (
+            (0, rows_of(2, 0, 2 * ROW), 0, rows_of(2, 0, 2 * ROW)),
+            (0, rows_of(2, 2 * ROW, 2 * ROW), 1, rows_of(2, 0, 2 * ROW)),
+        ),
+        ((2, 4 * ROW, CH),),
+        (above, below),
+        pl.ANY,
+    )
+    edges = moved(packed, TM, -1)
     taps_second = toeplitz(weight_second)
-    low = spread_mid(above, up, below, s2, taps_second, band, bands, ())
+    low = spread_mid(above, up_near, below, s2_near, taps_second, bands, ())
     mid_later = moved(low, TM, -1)
-    taps_first = toeplitz(after(weight_first, low))
     high = spread_mid(
-        above, up, below, after(s2, taps_first), taps_second, band, bands, (edges, later)
-    )
-    second, partial = sums(above, up, below, edges, later, s2, low, high, s1, planes, depth)
-    kept, sent = kept_and_sent(core, partial, mid_later, s1, second)
+        above, up_near, below, s2_near, taps_second, bands, (edges, later)
+    )
+    second, partial = sums(above, up_near, below, edges, later, s2_near, low, high, s1, planes, depth)
+    kept, sent = kept_and_sent(partial, mid_later, s1, second)
     received = lax.ppermute(sent, "core", [(0, 1), (1, 0)])
-    half = (kept.astype(F32) + received.astype(F32)).astype(BF16)
+    half = added(kept, received)
     part = exchanged(half, PLANE)
     part = part.astype(F32).sum(axis=0).astype(BF16)
-    grad_input = spread_all(low, high, mid_later, s1, taps_first)
-    part = exchanged(part.reshape(depth, PAD, CH), "z").astype(F32).sum(axis=0)
-    factor = 1.0 / math.sqrt(
-        frames * lax.axis_size(TM) * height * lax.axis_size(ROWS) * width
-    )
-    every = exchanged(jnp.broadcast_to(part * factor, (lax.axis_size(ROWS), PAD, CH)), ROWS)
-    every = every.reshape(-1, 2, PAD, CH)
-    share = weight_first.shape[0] // lax.axis_size(TM)
-    share_first, share_second = (every[:, c].reshape(-1, CH)[:share] for c in range(2))
+    grad_input = spread_all(low, high, mid_later, s1, weight_first)
+    part = exchanged(part.reshape(depth, PAD, CH), "z")
+    factor = 1.0 / math.sqrt(frames * lax.axis_size(TM) * height * bands * width)
+    every = exchanged(summed_copies(part, bands, factor), ROWS)
+    share_first, share_second = shares(every, weight_first.shape[0] // lax.axis_size(TM))
     return (grad_input.reshape(upstream.shape), share_first, share_second)
 
 

time: 141 us -> 131 us (0.929)
  local copies, waits for them, and re-layouts: 14.1 us -> 1.17 us
  waiting for transfers between devices: 32.5 us -> 36.9 us
  other arithmetic: 3.24 us -> 1.37 us
  Pallas kernels: 28 us -> 29.8 us
  starting transfers between devices: 18.3 us -> 16.8 us
    slice x8 -> x0, local copies, waits for them, and re-layouts: 6.23 us -> none  [the longest x3 2.29 us: body(): every[:, c].reshape(-1, CH)[:share]]
    unnamed x30 -> x6, local copies, waits for them, and re-layouts: 7.13 us -> 1.17 us
    ppermute x5, waiting for transfers between devices: 29.9 us -> 34.3 us  [moved(): return lax.ppermute(block, axis, route)]
    pallas_call x7 -> x11, Pallas kernels: 28 us -> 29.8 us  [the longest x9 27.5 us: local_call(): pl.pallas_call(kernel, out_shape=outs, in_specs=specs, scratch_shapes=scr...]
    concatenate x3 -> x0, other arithmetic: 1.57 us -> none  [the longest x1 0.78 us: body(): jnp.concatenate([up[:, :2 * ROW], s2[:, :ROW]], axis=1)]
  transfers between devices with their start and end apart: 7 -> 7, of which waited for: 4 -> 5; matrix products, arithmetic and copies ran while one was open for 2% -> 0% of each run, Pallas kernels for 16% -> 15%
where the time goes in v1:
time: 131 us; the launch traced here: 130 us
  blocking collectives  43.6 us (33%)
  waiting for transfers between devices  36.9 us (28%)
  Pallas kernels  29.8 us (23%)
  starting transfers between devices  16.8 us (13%)
  other arithmetic  1.37 us (1%)
    all_to_all x2, blocking collectives, exchanged(): return lax.all_to_all(pieces, axis, split_axis=0, concat_axis=0, tiled=True)  43.6 us
    ppermute x5, waiting for transfers between devices, moved(): return lax.ppermute(block, axis, route)  34.3 us
    pallas_call x9, Pallas kernels, local_call(): pl.pallas_call(kernel, out_shape=outs, in_specs=specs, scratch_shapes=scr...  27.5 us
    ppermute x5, starting transfers between devices, moved(): return lax.ppermute(block, axis, route)  10.4 us
    all_to_all x1, starting transfers between devices, exchanged(): return lax.all_to_all(pieces, axis, split_axis=0, concat_axis=0, tiled=True)  6.26 us
    ppermute x1, waiting for transfers between devices, body(): received = lax.ppermute(sent, 'core', [(0, 1), (1, 0)])  2.65 us
  transfers between devices with their start and end apart: 7, of which 5 were waited for; matrix products, arithmetic and copies ran while one was open for 0% of the time, Pallas kernels for 15%

profile of v1, /device:TPU:1, one launch (start us, length us, event | category | flops | bytes accessed | tf_op | source)
XLA Modules:
  0.0 130.4 jit_solution(4524697742220211302)
XLA Ops:
  0.6 2.1 %shard_map.76 = (bf16[4,384,128]{2,1,0:T(8,128)(2,1)S(1)}, bf16[4,384,128]{2,1,0:T(8,128)(2,1)S(1)}, bf16[2,1024,128]{2,1,0:T(8,128)(2,1)S(1)}, bf16[4,1024,128]...) custom-call(bf16[4,1024,128]{2,1,0:T(8,128)(2,1)} %bitcast.9, bf16[4,1024,128]{2,1,0:T(8,128)(2,1)} %bitcast.10), custom_call_target="tpu_custom_call" | custom-call | tf_op jit(solution)/shard_map/pallas_call | solution.py:48
  2.7 4.5 %collective-permute-start = (bf16[4,384,128]{2,1,0:T(8,128)(2,1)S(1)}, bf16[4,384,128]{2,1,0:T(8,128)(2,1)S(1)}, u32[]{:S(2)}, u32[]{:S(2)}) collective-permute-start(bf16[4,384,128]{2,1,0:T(8,128)(2,1)S(1)} %get-tuple-element.14), channel_id=1, source_target_pairs={{0,1},{1,2},{2,3},{3,4},{4,5},{5,6},{6,7},{7,8},{8,9},{9,10},{10,1... | collective-permute-start | bytes 1179656 | tf_op jit(solution)/shard_map/ppermute | solution.py:348
  7.3 1.9 %collective-permute-start.1 = (bf16[4,384,128]{2,1,0:T(8,128)(2,1)S(1)}, bf16[4,384,128]{2,1,0:T(8,128)(2,1)S(1)}, u32[]{:S(2)}, u32[]{:S(2)}) collective-permute-start(bf16[4,384,128]{2,1,0:T(8,128)(2,1)S(1)} %get-tuple-element.16), channel_id=1, source_target_pairs={{1,0},{2,1},{3,2},{4,3},{5,4},{6,5},{7,6},{8,7},{9,8},{10,9},{11,1... | collective-permute-start | bytes 1179656 | tf_op jit(solution)/shard_map/ppermute | solution.py:348
  9.2 0.4 shard_map.77.taps
  9.6 2.4 %collective-permute-done.above.refs_0_ = bf16[4,384,128]{2,1,0:T(8,128)(2,1)S(1)} collective-permute-done((bf16[4,384,128]{2,1,0:T(8,128)(2,1)S(1)}, bf16[4,384,128]{2,1,0:T(8,128)(2,1)S(1)}, u32[]{:S(2)}, u32[]{:S(2)}) %collective-permute-start) | collective-permute-done | bytes 393248 | tf_op jit(solution)/shard_map/ppermute | solution.py:348
  12.0 4.4 %collective-permute-done.1.below.refs_1_ = bf16[4,384,128]{2,1,0:T(8,128)(2,1)S(1)} collective-permute-done((bf16[4,384,128]{2,1,0:T(8,128)(2,1)S(1)}, bf16[4,384,128]{2,1,0:T(8,128)(2,1)S(1)}, u32[]{:S(2)}, u32[]{:S(2)}) %collective-permute-start.1) | collective-permute-done | bytes 393248 | tf_op jit(solution)/shard_map/ppermute | solution.py:348
  16.3 4.3 %shard_map.78.low = bf16[2,1280,128]{2,1,0:T(8,128)(2,1)S(1)} custom-call(bf16[4,384,128]{2,1,0:T(8,128)(2,1)S(1)} %collective-permute-done.above.refs_0_, bf16[4,1024,128]{2,1,0:T(8,128)(2,1)S(1)} %get-tuple-element.15.own.up, bf16[4,384,128]{2,1,0:T(8,128)(2,1)S(1)} %collective-permute-done.1.below.refs_1_, ...), custom_call_target="tpu_custom_call" | custom-call | tf_op jit(solution)/shard_map/pallas_call | solution.py:27
  20.6 1.3 collective-permute-start.4
  21.9 1.3 collective-permute-start.3
  23.4 1.4 %collective-permute-start.2 = (bf16[2,512,128]{2,1,0:T(8,128)(2,1)S(1)}, bf16[2,512,128]{2,1,0:T(8,128)(2,1)S(1)}, u32[]{:S(2)}, u32[]{:S(2)}) collective-permute-start(bf16[2,512,128]{2,1,0:T(8,128)(2,1)S(1)} %shard_map.79), channel_id=1, source_target_pairs={{16,0},{32,16},{48,32},{64,48},{80,64},{96,80},{112,96},{128,112},... | collective-permute-start | bytes 786440 | tf_op jit(solution)/shard_map/ppermute | solution.py:348
  24.9 24.7 %collective-permute-done.3.rest_1_.later = bf16[2,1024,128]{2,1,0:T(8,128)(2,1)S(1)} collective-permute-done((bf16[2,1024,128]{2,1,0:T(8,128)(2,1)S(1)}, bf16[2,1024,128]{2,1,0:T(8,128)(2,1)S(1)}, u32[]{:S(2)}, u32[]{:S(2)}) %collective-permute-start.3) | collective-permute-done | bytes 524320 | tf_op jit(solution)/shard_map/ppermute | solution.py:348
  49.5 2.8 %collective-permute-done.2.rest_0_.edges = bf16[2,512,128]{2,1,0:T(8,128)(2,1)S(1)} collective-permute-done((bf16[2,512,128]{2,1,0:T(8,128)(2,1)S(1)}, bf16[2,512,128]{2,1,0:T(8,128)(2,1)S(1)}, u32[]{:S(2)}, u32[]{:S(2)}) %collective-permute-start.2) | collective-permute-done | bytes 262176 | tf_op jit(solution)/shard_map/ppermute | solution.py:348
  52.3 4.5 %shard_map.80.high = bf16[2,1280,128]{2,1,0:T(8,128)(2,1)S(1)} custom-call(bf16[4,384,128]{2,1,0:T(8,128)(2,1)S(1)} %collective-permute-done.above.refs_0_, bf16[4,1024,128]{2,1,0:T(8,128)(2,1)S(1)} %get-tuple-element.15.own.up, bf16[4,384,128]{2,1,0:T(8,128)(2,1)S(1)} %collective-permute-done.1.below.refs_1_, ...), custom_call_target="tpu_custom_call" | custom-call | tf_op jit(solution)/shard_map/pallas_call | solution.py:27
  56.8 8.8 %shard_map.82 = (bf16[16,256,128]{2,1,0:T(8,128)(2,1)S(1)}, f32[384,1152]{1,0:T(8,128)S(1)}) custom-call(bf16[4,384,128]{2,1,0:T(8,128)(2,1)S(1)} %collective-permute-done.above.refs_0_, bf16[4,1024,128]{2,1,0:T(8,128)(2,1)S(1)} %get-tuple-element.15.own.up, bf16[4,384,128]{2,1,0:T(8,128)(2,1)S(1)} %collective-permute-done.1.below.refs_1_, ...), custom_call_target="tpu_custom_call" | custom-call | tf_op jit(solution)/shard_map/pallas_call | solution.py:27
  65.6 1.6 %shard_map.83 = (bf16[16,256,128]{2,1,0:T(8,128)(2,1)S(1)}, bf16[16,256,128]{2,1,0:T(8,128)(2,1)S(1)}) custom-call(f32[384,1152]{1,0:T(8,128)S(1)} %get-tuple-element.19.partial, bf16[2,1280,128]{2,1,0:T(8,128)(2,1)S(1)} %collective-permute-done.4.later, bf16[4,1024,128]{2,1,0:T(8,128)(2,1)S(1)} %bitcast.6, bf16[16,256,128]{2,1,0:T(8,128)(2,1)S(1)} %get-tuple-element.20.second), custom_call_target="tpu_custom_call" | custom-call | tf_op jit(solution)/shard_map/pallas_call | solution.py:27
  67.3 2.6 %collective-permute-done.5.other = bf16[16,256,128]{2,1,0:T(8,128)(2,1)S(1)} collective-permute-done((bf16[16,256,128]{2,1,0:T(8,128)(2,1)S(1)}, bf16[16,256,128]{2,1,0:T(8,128)(2,1)S(1)}, u32[]{:S(2)}, u32[]{:S(2)}) %collective-permute-start.5) | collective-permute-done | bytes 1048608 | tf_op jit(solution)/shard_map/ppermute | solution.py:399
  70.2 28.2 %all_to_all.15 = bf16[16,256,128]{2,1,0:T(8,128)(2,1)} all-to-all(bf16[16,256,128]{2,1,0:T(8,128)(2,1)S(1)} %shard_map.84), channel_id=1, replica_groups=mesh['z'=8,'yh'=2,'yl'=2,'x'=4,'core'=2] {'yh','yl','x'}, dimensions={0} | all-to-all | bytes 2097152 | tf_op jit(solution)/shard_map/all_to_all | solution.py:352
  98.5 1.4 %reduce_sum.12 = bf16[256,128]{1,0:T(8,128)(2,1)S(1)} reduce(bf16[16,256,128]{2,1,0:T(8,128)(2,1)} %all_to_all.15, bf16[]{:T(256)} %constant.2.clone.1), dimensions={0}, to_apply=%region_0.0 | reduce | flops 491520 | bytes 1114114 | tf_op jit(solution)/shard_map/reduce_sum | solution.py:402
  99.8 15.3 %all_to_all.16.pieces = bf16[8,32,128]{2,1,0:T(8,128)(2,1)S(1)} all-to-all(bf16[8,32,128]{2,1,0:T(8,128)(2,1)S(1)} %bitcast.11), channel_id=1, replica_groups=mesh['z'=8,'yh'=2,'yl'=2,'x'=4,'core'=2] {'z'}, dimensions={0} | all-to-all | bytes 131072 | tf_op jit(solution)/shard_map/all_to_all | solution.py:352
  115.1 0.7 shard_map.85
  115.9 6.3 %all-to-all-start.2 = ((f32[16,32,128]{2,1,0:T(8,128)}), f32[16,32,128]{2,1,0:T(8,128)S(1)}, u32[]{:S(2)}, u32[]{:S(2)}) async-start(f32[16,32,128]{2,1,0:T(8,128)} %shard_map.85), calls=%async_computation.2 | async-start | bytes 524288 | tf_op jit(solution)/shard_map/all_to_all | solution.py:352
  122.1 1.2 copy-done.2
  123.3 6.4 %shard_map.81 = bf16[4,1024,128]{2,1,0:T(8,128)(2,1)} custom-call(bf16[2,1280,128]{2,1,0:T(8,128)(2,1)S(1)} %shard_map.78.low, bf16[2,1280,128]{2,1,0:T(8,128)(2,1)S(1)} %shard_map.80.high, bf16[2,1280,128]{2,1,0:T(8,128)(2,1)S(1)} %collective-permute-done.4.later, bf16[4,1024,128]{2,1,0:T(8,128)(2,1)S(1)} %bitcast.7, bf16[3456,128]{1,0:T(8,128)(2,1)S(1)} %copy-done.2), custom_call_target="tpu_custom_call" | custom-call | tf_op jit(solution)/shard_map/pallas_call | solution.py:27
  129.7 0.7 shard_map.86
  (10 shorter events, 0.5 us)
Async XLA Ops:
  0.6 8.6 %copy-start.1 = (bf16[3456,128]{1,0:T(8,128)(2,1)S(1)}, bf16[3456,128]{1,0:T(8,128)(2,1)}, u32[]{:S(2)}) copy-start(bf16[3456,128]{1,0:T(8,128)(2,1)} %weight.2) | copy-start | bytes 2654212
  2.7 9.2 %collective-permute-start = (bf16[4,384,128]{2,1,0:T(8,128)(2,1)S(1)}, bf16[4,384,128]{2,1,0:T(8,128)(2,1)S(1)}, u32[]{:S(2)}, u32[]{:S(2)}) collective-permute-start(bf16[4,384,128]{2,1,0:T(8,128)(2,1)S(1)} %get-tuple-element.14), channel_id=1, source_target_pairs={{0,1},{1,2},{2,3},{3,4},{4,5},{5,6},{6,7},{7,8},{8,9},{9,10},{10,1... | collective-permute-start | bytes 1179656 | tf_op jit(solution)/shard_map/ppermute | solution.py:348
  7.3 9.1 %collective-permute-start.1 = (bf16[4,384,128]{2,1,0:T(8,128)(2,1)S(1)}, bf16[4,384,128]{2,1,0:T(8,128)(2,1)S(1)}, u32[]{:S(2)}, u32[]{:S(2)}) collective-permute-start(bf16[4,384,128]{2,1,0:T(8,128)(2,1)S(1)} %get-tuple-element.16), channel_id=1, source_target_pairs={{1,0},{2,1},{3,2},{4,3},{5,4},{6,5},{7,6},{8,7},{9,8},{10,9},{11,1... | collective-permute-start | bytes 1179656 | tf_op jit(solution)/shard_map/ppermute | solution.py:348
  20.6 45.0 %collective-permute-start.4 = (bf16[2,1280,128]{2,1,0:T(8,128)(2,1)S(1)}, bf16[2,1280,128]{2,1,0:T(8,128)(2,1)S(1)}, u32[]{:S(2)}, u32[]{:S(2)}) collective-permute-start(bf16[2,1280,128]{2,1,0:T(8,128)(2,1)S(1)} %shard_map.78.low), channel_id=1, source_target_pairs={{16,0},{32,16},{48,32},{64,48},{80,64},{96,80},{112,96},{128,112},... | collective-permute-start | bytes 1966088 | tf_op jit(solution)/shard_map/ppermute | solution.py:348
  21.9 27.6 %collective-permute-start.3 = (bf16[2,1024,128]{2,1,0:T(8,128)(2,1)S(1)}, bf16[2,1024,128]{2,1,0:T(8,128)(2,1)S(1)}, u32[]{:S(2)}, u32[]{:S(2)}) collective-permute-start(bf16[2,1024,128]{2,1,0:T(8,128)(2,1)S(1)} %get-tuple-element.18), channel_id=1, source_target_pairs={{16,0},{32,16},{48,32},{64,48},{80,64},{96,80},{112,96},{128,112},... | collective-permute-start | bytes 1572872 | tf_op jit(solution)/shard_map/ppermute | solution.py:348
  23.4 33.4 %copy-start = (bf16[4,8,128,128]{3,2,1,0:T(8,128)(2,1)S(1)}, bf16[4,8,128,128]{3,2,1,0:T(8,128)(2,1)}, u32[]{:S(2)}) copy-start(bf16[4,8,128,128]{3,2,1,0:T(8,128)(2,1)} %param.6) | copy-start | bytes 3145732
  23.4 28.9 %collective-permute-start.2 = (bf16[2,512,128]{2,1,0:T(8,128)(2,1)S(1)}, bf16[2,512,128]{2,1,0:T(8,128)(2,1)S(1)}, u32[]{:S(2)}, u32[]{:S(2)}) collective-permute-start(bf16[2,512,128]{2,1,0:T(8,128)(2,1)S(1)} %shard_map.79), channel_id=1, source_target_pairs={{16,0},{32,16},{48,32},{64,48},{80,64},{96,80},{112,96},{128,112},... | collective-permute-start | bytes 786440 | tf_op jit(solution)/shard_map/ppermute | solution.py:348
  67.2 2.7 %collective-permute-start.5 = (bf16[16,256,128]{2,1,0:T(8,128)(2,1)S(1)}, bf16[16,256,128]{2,1,0:T(8,128)(2,1)S(1)}, u32[]{:S(2)}, u32[]{:S(2)}) collective-permute-start(bf16[16,256,128]{2,1,0:T(8,128)(2,1)S(1)} %get-tuple-element.22), channel_id=1, source_target_pairs={{0,1},{1,0},{2,3},{3,2},{4,5},{5,4},{6,7},{7,6},{8,9},{9,8},{10,11... | collective-permute-start | bytes 3145736 | tf_op jit(solution)/shard_map/ppermute | solution.py:399
  115.9 13.8 %all-to-all-start.2 = ((f32[16,32,128]{2,1,0:T(8,128)}), f32[16,32,128]{2,1,0:T(8,128)S(1)}, u32[]{:S(2)}, u32[]{:S(2)}) async-start(f32[16,32,128]{2,1,0:T(8,128)} %shard_map.85), calls=%async_computation.2 | async-start | bytes 524288 | tf_op jit(solution)/shard_map/all_to_all | solution.py:352
  122.1 1.2 copy-start.2

commit v2 on v1

--- a/solution.py
+++ b/solution.py
@@ -278,16 +278,35 @@
 TOTAL = (3 * CH, 9 * CH)
 
 
-def sums(above, up, below, edges, later, saved_second, low, high, saved_first, planes, depth):
+def sum_here(above, up, below, saved):
+    positions = saved.shape[1]
+
+    def kernel(above, up, below, saved, total, wide, acts):
+        store_acts(acts, saved, range(4))
+        store_frames(wide, [with_rows(above, up, below, f, f, 1) for f in range(4)])
+        total[...] = jnp.zeros(TOTAL, F32)
+        add_products(total, acts, wide, 4, 0, 0, 4)
+
+    return local_call(
+        kernel,
+        jax.ShapeDtypeStruct(TOTAL, F32),
+        [
+            pltpu.VMEM((4 * (positions + 2 * ROW), 3 * CH), BF16),
+            pltpu.VMEM((4 * CH, positions), BF16),
+        ],
+        14,
+        above, up, below, saved,
+    )
+
+
+def sums(here, edges, later, saved_second, low, high, saved_first, planes, depth):
     positions = saved_first.shape[1]
-    stride = positions + 2 * ROW
-
-    def kernel(above, up, below, edges, later, s2, low, high, s1, share, partial, wide, acts, acts_first, total):
-        store_acts(acts, s2, range(4))
-        store_frames(wide, [with_rows(above, up, below, f, f, 1) for f in range(4)])
-        store_frames(wide, [next_frame(edges, later, f, 1) for f in range(2)], 4)
-        total[...] = jnp.zeros(TOTAL, F32)
-        add_products(total, acts, wide, 6, 0, 0, 4)
+
+    def kernel(here, edges, later, s2, low, high, s1, share, partial, wide, near, acts, acts_first, total):
+        store_acts(acts, s2, (2, 3))
+        store_frames(near, [next_frame(edges, later, f, 1) for f in range(2)])
+        total[...] = here[...]
+        add_products(total, acts, near, 2, 4, 2, 2)
         store_share(share, total)
         store_acts(acts_first, s1, range(4))
         store_frames(wide, [whole(ref, f) for ref in (low, high) for f in range(2)])
@@ -301,13 +320,14 @@
             jax.ShapeDtypeStruct(TOTAL, F32),
         ),
         [
-            pltpu.VMEM((6 * stride, 3 * CH), BF16),
-            pltpu.VMEM((4 * CH, positions), BF16),
+            pltpu.VMEM((4 * low.shape[1], 3 * CH), BF16),
+            pltpu.VMEM((2 * low.shape[1], 3 * CH), BF16),
+            pltpu.VMEM((2 * CH, positions), BF16),
             pltpu.VMEM((4 * CH, positions), BF16),
             pltpu.VMEM(TOTAL, F32),
         ],
-        16,
-        above, up, below, edges, later, saved_second, low, high, saved_first,
+        18,
+        here, edges, later, saved_second, low, high, saved_first,
     )
 
 
@@ -391,10 +411,11 @@
     taps_second = toeplitz(weight_second)
     low = spread_mid(above, up_near, below, s2_near, taps_second, bands, ())
     mid_later = moved(low, TM, -1)
+    here = sum_here(above, up_near, below, s2_near)
     high = spread_mid(
         above, up_near, below, s2_near, taps_second, bands, (edges, later)
     )
-    second, partial = sums(above, up_near, below, edges, later, s2_near, low, high, s1, planes, depth)
+    second, partial = sums(here, edges, later, s2_near, low, high, s1, planes, depth)
     kept, sent = kept_and_sent(partial, mid_later, s1, second)
     received = lax.ppermute(sent, "core", [(0, 1), (1, 0)])
     half = added(kept, received)

time: 131 us -> 127 us (0.969)
  waiting for transfers between devices: 36.9 us -> 33.5 us
    ppermute x5, waiting for transfers between devices: 34.3 us -> 30.9 us  [moved(): return lax.ppermute(block, axis, route)]
    pallas_call x9 -> x10, Pallas kernels: 27.5 us -> 27.1 us  [local_call(): pl.pallas_call(kernel, out_shape=outs, in_specs=specs, scratch_shapes=scr...]
  transfers between devices with their start and end apart: 7 -> 7, of which waited for: 5 -> 5; matrix products, arithmetic and copies ran while one was open for 0% -> 0% of each run, Pallas kernels for 15% -> 16%
where the time goes in v2:
time: 127 us; the launch traced here: 126 us
  blocking collectives  43.6 us (34%)
  waiting for transfers between devices  33.5 us (26%)
  Pallas kernels  29.4 us (23%)
  starting transfers between devices  16.6 us (13%)
  other arithmetic  1.37 us (1%)
    all_to_all x2, blocking collectives, exchanged(): return lax.all_to_all(pieces, axis, split_axis=0, concat_axis=0, tiled=True)  43.6 us
    ppermute x5, waiting for transfers between devices, moved(): return lax.ppermute(block, axis, route)  30.9 us
    pallas_call x10, Pallas kernels, local_call(): pl.pallas_call(kernel, out_shape=outs, in_specs=specs, scratch_shapes=scr...  27.1 us
    ppermute x5, starting transfers between devices, moved(): return lax.ppermute(block, axis, route)  10.3 us
    all_to_all x1, starting transfers between devices, exchanged(): return lax.all_to_all(pieces, axis, split_axis=0, concat_axis=0, tiled=True)  6.25 us
    ppermute x1, waiting for transfers between devices, body(): received = lax.ppermute(sent, 'core', [(0, 1), (1, 0)])  2.65 us
  transfers between devices with their start and end apart: 7, of which 5 were waited for; matrix products, arithmetic and copies ran while one was open for 0% of the time, Pallas kernels for 16%

profile of v2, /device:TPU:1, one launch (start us, length us, event | category | flops | bytes accessed | tf_op | source)
XLA Modules:
  0.0 126.4 jit_solution(11563618687498652714)
XLA Ops:
  0.6 2.1 %shard_map.76 = (bf16[4,384,128]{2,1,0:T(8,128)(2,1)S(1)}, bf16[4,384,128]{2,1,0:T(8,128)(2,1)S(1)}, bf16[2,1024,128]{2,1,0:T(8,128)(2,1)S(1)}, bf16[4,1024,128]...) custom-call(bf16[4,1024,128]{2,1,0:T(8,128)(2,1)} %bitcast.9, bf16[4,1024,128]{2,1,0:T(8,128)(2,1)} %bitcast.10), custom_call_target="tpu_custom_call" | custom-call | tf_op jit(solution)/shard_map/pallas_call | solution.py:48
  2.7 4.5 %collective-permute-start = (bf16[4,384,128]{2,1,0:T(8,128)(2,1)S(1)}, bf16[4,384,128]{2,1,0:T(8,128)(2,1)S(1)}, u32[]{:S(2)}, u32[]{:S(2)}) collective-permute-start(bf16[4,384,128]{2,1,0:T(8,128)(2,1)S(1)} %get-tuple-element.14), channel_id=1, source_target_pairs={{0,1},{1,2},{2,3},{3,4},{4,5},{5,6},{6,7},{7,8},{8,9},{9,10},{10,1... | collective-permute-start | bytes 1179656 | tf_op jit(solution)/shard_map/ppermute | solution.py:368
  7.3 1.9 %collective-permute-start.1 = (bf16[4,384,128]{2,1,0:T(8,128)(2,1)S(1)}, bf16[4,384,128]{2,1,0:T(8,128)(2,1)S(1)}, u32[]{:S(2)}, u32[]{:S(2)}) collective-permute-start(bf16[4,384,128]{2,1,0:T(8,128)(2,1)S(1)} %get-tuple-element.16), channel_id=1, source_target_pairs={{1,0},{2,1},{3,2},{4,3},{5,4},{6,5},{7,6},{8,7},{9,8},{10,9},{11,1... | collective-permute-start | bytes 1179656 | tf_op jit(solution)/shard_map/ppermute | solution.py:368
  9.6 2.4 %collective-permute-done.above.refs_0_ = bf16[4,384,128]{2,1,0:T(8,128)(2,1)S(1)} collective-permute-done((bf16[4,384,128]{2,1,0:T(8,128)(2,1)S(1)}, bf16[4,384,128]{2,1,0:T(8,128)(2,1)S(1)}, u32[]{:S(2)}, u32[]{:S(2)}) %collective-permute-start) | collective-permute-done | bytes 393248 | tf_op jit(solution)/shard_map/ppermute | solution.py:368
  12.0 4.4 %collective-permute-done.1.below.refs_1_ = bf16[4,384,128]{2,1,0:T(8,128)(2,1)S(1)} collective-permute-done((bf16[4,384,128]{2,1,0:T(8,128)(2,1)S(1)}, bf16[4,384,128]{2,1,0:T(8,128)(2,1)S(1)}, u32[]{:S(2)}, u32[]{:S(2)}) %collective-permute-start.1) | collective-permute-done | bytes 393248 | tf_op jit(solution)/shard_map/ppermute | solution.py:368
  16.3 4.3 %shard_map.78.low = bf16[2,1280,128]{2,1,0:T(8,128)(2,1)S(1)} custom-call(bf16[4,384,128]{2,1,0:T(8,128)(2,1)S(1)} %collective-permute-done.above.refs_0_, bf16[4,1024,128]{2,1,0:T(8,128)(2,1)S(1)} %get-tuple-element.15.own.up, bf16[4,384,128]{2,1,0:T(8,128)(2,1)S(1)} %collective-permute-done.1.below.refs_1_, ...), custom_call_target="tpu_custom_call" | custom-call | tf_op jit(solution)/shard_map/pallas_call | solution.py:27
  20.6 1.3 %collective-permute-start.4 = (bf16[2,1280,128]{2,1,0:T(8,128)(2,1)S(1)}, bf16[2,1280,128]{2,1,0:T(8,128)(2,1)S(1)}, u32[]{:S(2)}, u32[]{:S(2)}) collective-permute-start(bf16[2,1280,128]{2,1,0:T(8,128)(2,1)S(1)} %shard_map.78.low), channel_id=1, source_target_pairs={{16,0},{32,16},{48,32},{64,48},{80,64},{96,80},{112,96},{128,112},... | collective-permute-start | bytes 1966088 | tf_op jit(solution)/shard_map/ppermute | solution.py:368
  21.9 1.3 %collective-permute-start.3 = (bf16[2,1024,128]{2,1,0:T(8,128)(2,1)S(1)}, bf16[2,1024,128]{2,1,0:T(8,128)(2,1)S(1)}, u32[]{:S(2)}, u32[]{:S(2)}) collective-permute-start(bf16[2,1024,128]{2,1,0:T(8,128)(2,1)S(1)} %get-tuple-element.18), channel_id=1, source_target_pairs={{16,0},{32,16},{48,32},{64,48},{80,64},{96,80},{112,96},{128,112},... | collective-permute-start | bytes 1572872 | tf_op jit(solution)/shard_map/ppermute | solution.py:368
  23.4 1.3 %collective-permute-start.2 = (bf16[2,512,128]{2,1,0:T(8,128)(2,1)S(1)}, bf16[2,512,128]{2,1,0:T(8,128)(2,1)S(1)}, u32[]{:S(2)}, u32[]{:S(2)}) collective-permute-start(bf16[2,512,128]{2,1,0:T(8,128)(2,1)S(1)} %shard_map.79), channel_id=1, source_target_pairs={{16,0},{32,16},{48,32},{64,48},{80,64},{96,80},{112,96},{128,112},... | collective-permute-start | bytes 786440 | tf_op jit(solution)/shard_map/ppermute | solution.py:368
  24.7 3.5 %shard_map.82.here = f32[384,1152]{1,0:T(8,128)S(1)} custom-call(bf16[4,384,128]{2,1,0:T(8,128)(2,1)S(1)} %collective-permute-done.above.refs_0_, bf16[4,1024,128]{2,1,0:T(8,128)(2,1)S(1)} %get-tuple-element.15.own.up, bf16[4,384,128]{2,1,0:T(8,128)(2,1)S(1)} %collective-permute-done.1.below.refs_1_, bf16[4,1024,128]{2,1,0:T(8,128)(2,1)S(1)} %get-tuple-element.17.saved.s2), custom_call_target="tpu_custom_call" | custom-call | tf_op jit(solution)/shard_map/pallas_call | solution.py:27
  28.3 21.3 %collective-permute-done.3.rest_1_.later = bf16[2,1024,128]{2,1,0:T(8,128)(2,1)S(1)} collective-permute-done((bf16[2,1024,128]{2,1,0:T(8,128)(2,1)S(1)}, bf16[2,1024,128]{2,1,0:T(8,128)(2,1)S(1)}, u32[]{:S(2)}, u32[]{:S(2)}) %collective-permute-start.3) | collective-permute-done | bytes 524320 | tf_op jit(solution)/shard_map/ppermute | solution.py:368
  49.5 2.8 %collective-permute-done.2.rest_0_.edges = bf16[2,512,128]{2,1,0:T(8,128)(2,1)S(1)} collective-permute-done((bf16[2,512,128]{2,1,0:T(8,128)(2,1)S(1)}, bf16[2,512,128]{2,1,0:T(8,128)(2,1)S(1)}, u32[]{:S(2)}, u32[]{:S(2)}) %collective-permute-start.2) | collective-permute-done | bytes 262176 | tf_op jit(solution)/shard_map/ppermute | solution.py:368
  52.3 4.5 %shard_map.80.high = bf16[2,1280,128]{2,1,0:T(8,128)(2,1)S(1)} custom-call(bf16[4,384,128]{2,1,0:T(8,128)(2,1)S(1)} %collective-permute-done.above.refs_0_, bf16[4,1024,128]{2,1,0:T(8,128)(2,1)S(1)} %get-tuple-element.15.own.up, bf16[4,384,128]{2,1,0:T(8,128)(2,1)S(1)} %collective-permute-done.1.below.refs_1_, ...), custom_call_target="tpu_custom_call" | custom-call | tf_op jit(solution)/shard_map/pallas_call | solution.py:27
  56.8 4.8 %shard_map.83 = (bf16[16,256,128]{2,1,0:T(8,128)(2,1)S(1)}, f32[384,1152]{1,0:T(8,128)S(1)}) custom-call(f32[384,1152]{1,0:T(8,128)S(1)} %shard_map.82.here, bf16[2,512,128]{2,1,0:T(8,128)(2,1)S(1)} %collective-permute-done.2.rest_0_.edges, bf16[2,1024,128]{2,1,0:T(8,128)(2,1)S(1)} %collective-permute-done.3.rest_1_.later, ...), custom_call_target="tpu_custom_call" | custom-call | tf_op jit(solution)/shard_map/pallas_call | solution.py:27
  61.6 1.6 %shard_map.84 = (bf16[16,256,128]{2,1,0:T(8,128)(2,1)S(1)}, bf16[16,256,128]{2,1,0:T(8,128)(2,1)S(1)}) custom-call(f32[384,1152]{1,0:T(8,128)S(1)} %get-tuple-element.19.partial, bf16[2,1280,128]{2,1,0:T(8,128)(2,1)S(1)} %collective-permute-done.4.later, bf16[4,1024,128]{2,1,0:T(8,128)(2,1)S(1)} %bitcast.6, bf16[16,256,128]{2,1,0:T(8,128)(2,1)S(1)} %get-tuple-element.20.second), custom_call_target="tpu_custom_call" | custom-call | tf_op jit(solution)/shard_map/pallas_call | solution.py:27
  63.3 2.6 %collective-permute-done.5.other = bf16[16,256,128]{2,1,0:T(8,128)(2,1)S(1)} collective-permute-done((bf16[16,256,128]{2,1,0:T(8,128)(2,1)S(1)}, bf16[16,256,128]{2,1,0:T(8,128)(2,1)S(1)}, u32[]{:S(2)}, u32[]{:S(2)}) %collective-permute-start.5) | collective-permute-done | bytes 1048608 | tf_op jit(solution)/shard_map/ppermute | solution.py:420
  66.2 28.2 %all_to_all.15 = bf16[16,256,128]{2,1,0:T(8,128)(2,1)} all-to-all(bf16[16,256,128]{2,1,0:T(8,128)(2,1)S(1)} %shard_map.85), channel_id=1, replica_groups=mesh['z'=8,'yh'=2,'yl'=2,'x'=4,'core'=2] {'yh','yl','x'}, dimensions={0} | all-to-all | bytes 2097152 | tf_op jit(solution)/shard_map/all_to_all | solution.py:372
  94.5 1.4 %reduce_sum.12 = bf16[256,128]{1,0:T(8,128)(2,1)S(1)} reduce(bf16[16,256,128]{2,1,0:T(8,128)(2,1)} %all_to_all.15, bf16[]{:T(256)} %constant.2.clone.1), dimensions={0}, to_apply=%region_0.0 | reduce | flops 491520 | bytes 1114114 | tf_op jit(solution)/shard_map/reduce_sum | solution.py:423
  95.8 15.3 %all_to_all.16.pieces = bf16[8,32,128]{2,1,0:T(8,128)(2,1)S(1)} all-to-all(bf16[8,32,128]{2,1,0:T(8,128)(2,1)S(1)} %bitcast.11), channel_id=1, replica_groups=mesh['z'=8,'yh'=2,'yl'=2,'x'=4,'core'=2] {'z'}, dimensions={0} | all-to-all | bytes 131072 | tf_op jit(solution)/shard_map/all_to_all | solution.py:372
  111.2 0.7 shard_map.86
  111.9 6.2 %all-to-all-start.2 = ((f32[16,32,128]{2,1,0:T(8,128)}), f32[16,32,128]{2,1,0:T(8,128)S(1)}, u32[]{:S(2)}, u32[]{:S(2)}) async-start(f32[16,32,128]{2,1,0:T(8,128)} %shard_map.86), calls=%async_computation.2 | async-start | bytes 524288 | tf_op jit(solution)/shard_map/all_to_all | solution.py:372
  118.2 1.2 copy-done.2
  119.3 6.4 %shard_map.81 = bf16[4,1024,128]{2,1,0:T(8,128)(2,1)} custom-call(bf16[2,1280,128]{2,1,0:T(8,128)(2,1)S(1)} %shard_map.78.low, bf16[2,1280,128]{2,1,0:T(8,128)(2,1)S(1)} %shard_map.80.high, bf16[2,1280,128]{2,1,0:T(8,128)(2,1)S(1)} %collective-permute-done.4.later, bf16[4,1024,128]{2,1,0:T(8,128)(2,1)S(1)} %bitcast.7, bf16[3456,128]{1,0:T(8,128)(2,1)S(1)} %copy-done.2), custom_call_target="tpu_custom_call" | custom-call | tf_op jit(solution)/shard_map/pallas_call | solution.py:27
  125.7 0.7 shard_map.87
  (11 shorter events, 0.9 us)
Async XLA Ops:
  0.6 8.6 %copy-start.1 = (bf16[3456,128]{1,0:T(8,128)(2,1)S(1)}, bf16[3456,128]{1,0:T(8,128)(2,1)}, u32[]{:S(2)}) copy-start(bf16[3456,128]{1,0:T(8,128)(2,1)} %weight.2) | copy-start | bytes 2654212
  2.7 9.2 %collective-permute-start = (bf16[4,384,128]{2,1,0:T(8,128)(2,1)S(1)}, bf16[4,384,128]{2,1,0:T(8,128)(2,1)S(1)}, u32[]{:S(2)}, u32[]{:S(2)}) collective-permute-start(bf16[4,384,128]{2,1,0:T(8,128)(2,1)S(1)} %get-tuple-element.14), channel_id=1, source_target_pairs={{0,1},{1,2},{2,3},{3,4},{4,5},{5,6},{6,7},{7,8},{8,9},{9,10},{10,1... | collective-permute-start | bytes 1179656 | tf_op jit(solution)/shard_map/ppermute | solution.py:368
  7.3 9.1 %collective-permute-start.1 = (bf16[4,384,128]{2,1,0:T(8,128)(2,1)S(1)}, bf16[4,384,128]{2,1,0:T(8,128)(2,1)S(1)}, u32[]{:S(2)}, u32[]{:S(2)}) collective-permute-start(bf16[4,384,128]{2,1,0:T(8,128)(2,1)S(1)} %get-tuple-element.16), channel_id=1, source_target_pairs={{1,0},{2,1},{3,2},{4,3},{5,4},{6,5},{7,6},{8,7},{9,8},{10,9},{11,1... | collective-permute-start | bytes 1179656 | tf_op jit(solution)/shard_map/ppermute | solution.py:368
  20.6 41.0 %collective-permute-start.4 = (bf16[2,1280,128]{2,1,0:T(8,128)(2,1)S(1)}, bf16[2,1280,128]{2,1,0:T(8,128)(2,1)S(1)}, u32[]{:S(2)}, u32[]{:S(2)}) collective-permute-start(bf16[2,1280,128]{2,1,0:T(8,128)(2,1)S(1)} %shard_map.78.low), channel_id=1, source_target_pairs={{16,0},{32,16},{48,32},{64,48},{80,64},{96,80},{112,96},{128,112},... | collective-permute-start | bytes 1966088 | tf_op jit(solution)/shard_map/ppermute | solution.py:368
  21.9 27.6 %collective-permute-start.3 = (bf16[2,1024,128]{2,1,0:T(8,128)(2,1)S(1)}, bf16[2,1024,128]{2,1,0:T(8,128)(2,1)S(1)}, u32[]{:S(2)}, u32[]{:S(2)}) collective-permute-start(bf16[2,1024,128]{2,1,0:T(8,128)(2,1)S(1)} %get-tuple-element.18), channel_id=1, source_target_pairs={{16,0},{32,16},{48,32},{64,48},{80,64},{96,80},{112,96},{128,112},... | collective-permute-start | bytes 1572872 | tf_op jit(solution)/shard_map/ppermute | solution.py:368
  23.4 28.9 %collective-permute-start.2 = (bf16[2,512,128]{2,1,0:T(8,128)(2,1)S(1)}, bf16[2,512,128]{2,1,0:T(8,128)(2,1)S(1)}, u32[]{:S(2)}, u32[]{:S(2)}) collective-permute-start(bf16[2,512,128]{2,1,0:T(8,128)(2,1)S(1)} %shard_map.79), channel_id=1, source_target_pairs={{16,0},{32,16},{48,32},{64,48},{80,64},{96,80},{112,96},{128,112},... | collective-permute-start | bytes 786440 | tf_op jit(solution)/shard_map/ppermute | solution.py:368
  28.3 28.6 %copy-start = (bf16[4,8,128,128]{3,2,1,0:T(8,128)(2,1)S(1)}, bf16[4,8,128,128]{3,2,1,0:T(8,128)(2,1)}, u32[]{:S(2)}) copy-start(bf16[4,8,128,128]{3,2,1,0:T(8,128)(2,1)} %param.6) | copy-start | bytes 3145732
  63.2 2.7 %collective-permute-start.5 = (bf16[16,256,128]{2,1,0:T(8,128)(2,1)S(1)}, bf16[16,256,128]{2,1,0:T(8,128)(2,1)S(1)}, u32[]{:S(2)}, u32[]{:S(2)}) collective-permute-start(bf16[16,256,128]{2,1,0:T(8,128)(2,1)S(1)} %get-tuple-element.22), channel_id=1, source_target_pairs={{0,1},{1,0},{2,3},{3,2},{4,5},{5,4},{6,7},{7,6},{8,9},{9,8},{10,11... | collective-permute-start | bytes 3145736 | tf_op jit(solution)/shard_map/ppermute | solution.py:420
  111.9 13.8 %all-to-all-start.2 = ((f32[16,32,128]{2,1,0:T(8,128)}), f32[16,32,128]{2,1,0:T(8,128)S(1)}, u32[]{:S(2)}, u32[]{:S(2)}) async-start(f32[16,32,128]{2,1,0:T(8,128)} %shard_map.86), calls=%async_computation.2 | async-start | bytes 524288 | tf_op jit(solution)/shard_map/all_to_all | solution.py:372
  118.1 1.2 copy-start.2

commit v3 on v2

--- a/solution.py
+++ b/solution.py
@@ -17,7 +17,8 @@
 CH = 128
 
 
-PAD = 32
+TILE = 8
+SLOTS = 4
 BLOCK = 512
 ROW = 128
 
@@ -79,12 +80,15 @@
 
 
 def shares(every, share):
+    chips, tiles = every.shape[0] // 2, share // TILE
+
     def kernel(every, first, second):
-        for out, core in ((first, 0), (second, 1)):
-            for chip in range(every.shape[0] // 2):
-                rows = min(PAD, share - chip * PAD)
-                if rows > 0:
-                    out[chip * PAD : chip * PAD + rows, :] = every[2 * chip + core, 0:rows, :]
+        z = lax.axis_index("z")
+        for k in range(tiles):
+            chip = lax.rem(tiles * z + k, chips)
+            rows = slice(k * TILE, (k + 1) * TILE)
+            first[rows, :] = every[2 * chip, k // chips]
+            second[rows, :] = every[2 * chip + 1, k // chips]
 
     out = jax.ShapeDtypeStruct((share, CH), F32)
     return local_call(kernel, (out, out), [], 8, every)
@@ -232,21 +236,42 @@
 
 
 def store_share(out, total):
-    planes, depth = out.shape[0], out.shape[1] // PAD
-    chips = planes // 2
-    share = 27 * CH // (2 * depth)
-    for z in range(depth):
-        for plane in range(planes):
-            block, chip = 2 * z + plane // chips, plane % chips
+    planes, rows = out.shape[0], out.shape[1]
+    chips, tiles = planes // 2, rows // TILE
+    for plane in range(planes):
+        half, chip = divmod(plane, chips)
+        for start in range(0, tiles, 4):
             values = []
-            for row in range(chip * PAD, (chip + 1) * PAD, 8):
-                if row < share:
-                    tap, line = divmod(block * share + row, CH)
-                    p, tap = divmod(tap, 9)
-                    values.append(total[p * CH + line : p * CH + line + 8, tap * CH : (tap + 1) * CH])
-                else:
-                    values.append(jnp.zeros((8, CH), F32))
-            out[plane, z * PAD : (z + 1) * PAD, :] = jnp.concatenate(values).astype(BF16)
+            for m in range(start, min(start + 4, tiles)):
+                z, k = divmod(chips * m + chip, tiles)
+                tap, line = divmod((2 * z + half) * rows + k * TILE, CH)
+                p, tap = divmod(tap, 9)
+                values.append(
+                    total[p * CH + line : p * CH + line + TILE, tap * CH : (tap + 1) * CH]
+                )
+            size = TILE * len(values)
+            out[plane, start * TILE : start * TILE + size, :] = jnp.concatenate(values).astype(BF16)
+
+
+def plane_sum(pieces, depth):
+    tiles = pieces.shape[1] // TILE
+    chips = pieces.shape[0] // 2
+
+    def kernel(pieces, out, total):
+        value = pieces[0].astype(F32)
+        for at in range(1, pieces.shape[0]):
+            value += pieces[at].astype(F32)
+        total[...] = value
+        out[...] = jnp.zeros(out.shape, BF16)
+        chip = lax.axis_index(("yl", "x"))
+        for m in range(tiles):
+            tile = chip + chips * m
+            z, k = lax.div(tile, tiles), lax.rem(tile, tiles)
+            out[z, lax.div(k, chips)] = total[m * TILE : (m + 1) * TILE, :].astype(BF16)
+
+    out = jax.ShapeDtypeStruct((depth, SLOTS, TILE, CH), BF16)
+    pieces = pltpu.with_memory_space_constraint(pieces, pltpu.HBM)
+    return local_call(kernel, out, [pltpu.VMEM(pieces.shape[1:], F32)], 8, pieces)
 
 
 def store_acts(turned, saved, frames):
@@ -299,7 +324,7 @@
     )
 
 
-def sums(here, edges, later, saved_second, low, high, saved_first, planes, depth):
+def sums(here, edges, later, saved_second, low, high, saved_first, planes):
     positions = saved_first.shape[1]
 
     def kernel(here, edges, later, s2, low, high, s1, share, partial, wide, near, acts, acts_first, total):
@@ -316,7 +341,7 @@
     return local_call(
         kernel,
         (
-            jax.ShapeDtypeStruct((planes, depth * PAD, CH), BF16),
+            jax.ShapeDtypeStruct((planes, 27 * CH // planes, CH), BF16),
             jax.ShapeDtypeStruct(TOTAL, F32),
         ),
         [
@@ -415,14 +440,14 @@
     high = spread_mid(
         above, up_near, below, s2_near, taps_second, bands, (edges, later)
     )
-    second, partial = sums(here, edges, later, s2_near, low, high, s1, planes, depth)
+    second, partial = sums(here, edges, later, s2_near, low, high, s1, planes)
     kept, sent = kept_and_sent(partial, mid_later, s1, second)
     received = lax.ppermute(sent, "core", [(0, 1), (1, 0)])
     half = added(kept, received)
     part = exchanged(half, PLANE)
-    part = part.astype(F32).sum(axis=0).astype(BF16)
+    part = plane_sum(part, depth)
     grad_input = spread_all(low, high, mid_later, s1, weight_first)
-    part = exchanged(part.reshape(depth, PAD, CH), "z")
+    part = exchanged(part, "z")
     factor = 1.0 / math.sqrt(frames * lax.axis_size(TM) * height * bands * width)
     every = exchanged(summed_copies(part, bands, factor), ROWS)
     share_first, share_second = shares(every, weight_first.shape[0] // lax.axis_size(TM))

time: 127 us -> 125 us (0.984)
  blocking collectives: 43.6 us -> 41.9 us
  other arithmetic: 1.37 us -> 0 us
    all_to_all x2, blocking collectives: 43.6 us -> 41.9 us  [exchanged(): return lax.all_to_all(pieces, axis, split_axis=0, concat_axis=0, tiled=True)]
    reduce_sum x1 -> x0, other arithmetic: 1.37 us -> none  [body(): part = part.astype(F32).sum(axis=0).astype(BF16)]
    pallas_call x10 -> x11, Pallas kernels: 27.1 us -> 28.3 us  [local_call(): pl.pallas_call(kernel, out_shape=outs, in_specs=specs, scratch_shapes=scr...]
where the time goes in v3:
time: 125 us; the launch traced here: 124 us
  blocking collectives  41.9 us (34%)
  waiting for transfers between devices  33.3 us (27%)
  Pallas kernels  30.6 us (24%)
  starting transfers between devices  16.5 us (13%)
    all_to_all x2, blocking collectives, exchanged(): return lax.all_to_all(pieces, axis, split_axis=0, concat_axis=0, tiled=True)  41.9 us
    ppermute x5, waiting for transfers between devices, moved(): return lax.ppermute(block, axis, route)  30.9 us
    pallas_call x11, Pallas kernels, local_call(): pl.pallas_call(kernel, out_shape=outs, in_specs=specs, scratch_shapes=scr...  28.3 us
    ppermute x5, starting transfers between devices, moved(): return lax.ppermute(block, axis, route)  10.3 us
    all_to_all x1, starting transfers between devices, exchanged(): return lax.all_to_all(pieces, axis, split_axis=0, concat_axis=0, tiled=True)  6.15 us
  transfers between devices with their start and end apart: 7, of which 5 were waited for; matrix products, arithmetic and copies ran while one was open for 0% of the time, Pallas kernels for 16%

profile of v3, /device:TPU:1, one launch (start us, length us, event | category | flops | bytes accessed | tf_op | source)
XLA Modules:
  0.0 124.3 jit_solution(17612024688110362167)
XLA Ops:
  0.6 2.1 %shard_map.76 = (bf16[4,384,128]{2,1,0:T(8,128)(2,1)S(1)}, bf16[4,384,128]{2,1,0:T(8,128)(2,1)S(1)}, bf16[2,1024,128]{2,1,0:T(8,128)(2,1)S(1)}, bf16[4,1024,128]...) custom-call(bf16[4,1024,128]{2,1,0:T(8,128)(2,1)} %bitcast.8, bf16[4,1024,128]{2,1,0:T(8,128)(2,1)} %bitcast.9), custom_call_target="tpu_custom_call" | custom-call | tf_op jit(solution)/shard_map/pallas_call | solution.py:49
  2.7 4.5 %collective-permute-start = (bf16[4,384,128]{2,1,0:T(8,128)(2,1)S(1)}, bf16[4,384,128]{2,1,0:T(8,128)(2,1)S(1)}, u32[]{:S(2)}, u32[]{:S(2)}) collective-permute-start(bf16[4,384,128]{2,1,0:T(8,128)(2,1)S(1)} %get-tuple-element.14), channel_id=1, source_target_pairs={{0,1},{1,2},{2,3},{3,4},{4,5},{5,6},{6,7},{7,8},{8,9},{9,10},{10,1... | collective-permute-start | bytes 1179656 | tf_op jit(solution)/shard_map/ppermute | solution.py:393
  7.3 1.9 %collective-permute-start.1 = (bf16[4,384,128]{2,1,0:T(8,128)(2,1)S(1)}, bf16[4,384,128]{2,1,0:T(8,128)(2,1)S(1)}, u32[]{:S(2)}, u32[]{:S(2)}) collective-permute-start(bf16[4,384,128]{2,1,0:T(8,128)(2,1)S(1)} %get-tuple-element.16), channel_id=1, source_target_pairs={{1,0},{2,1},{3,2},{4,3},{5,4},{6,5},{7,6},{8,7},{9,8},{10,9},{11,1... | collective-permute-start | bytes 1179656 | tf_op jit(solution)/shard_map/ppermute | solution.py:393
  9.6 2.4 %collective-permute-done.above.refs_0_ = bf16[4,384,128]{2,1,0:T(8,128)(2,1)S(1)} collective-permute-done((bf16[4,384,128]{2,1,0:T(8,128)(2,1)S(1)}, bf16[4,384,128]{2,1,0:T(8,128)(2,1)S(1)}, u32[]{:S(2)}, u32[]{:S(2)}) %collective-permute-start) | collective-permute-done | bytes 393248 | tf_op jit(solution)/shard_map/ppermute | solution.py:393
  12.0 4.4 %collective-permute-done.1.below.refs_1_ = bf16[4,384,128]{2,1,0:T(8,128)(2,1)S(1)} collective-permute-done((bf16[4,384,128]{2,1,0:T(8,128)(2,1)S(1)}, bf16[4,384,128]{2,1,0:T(8,128)(2,1)S(1)}, u32[]{:S(2)}, u32[]{:S(2)}) %collective-permute-start.1) | collective-permute-done | bytes 393248 | tf_op jit(solution)/shard_map/ppermute | solution.py:393
  16.3 4.3 %shard_map.78.low = bf16[2,1280,128]{2,1,0:T(8,128)(2,1)S(1)} custom-call(bf16[4,384,128]{2,1,0:T(8,128)(2,1)S(1)} %collective-permute-done.above.refs_0_, bf16[4,1024,128]{2,1,0:T(8,128)(2,1)S(1)} %get-tuple-element.15.own.up, bf16[4,384,128]{2,1,0:T(8,128)(2,1)S(1)} %collective-permute-done.1.below.refs_1_, ...), custom_call_target="tpu_custom_call" | custom-call | tf_op jit(solution)/shard_map/pallas_call | solution.py:28
  20.6 1.3 %collective-permute-start.4 = (bf16[2,1280,128]{2,1,0:T(8,128)(2,1)S(1)}, bf16[2,1280,128]{2,1,0:T(8,128)(2,1)S(1)}, u32[]{:S(2)}, u32[]{:S(2)}) collective-permute-start(bf16[2,1280,128]{2,1,0:T(8,128)(2,1)S(1)} %shard_map.78.low), channel_id=1, source_target_pairs={{16,0},{32,16},{48,32},{64,48},{80,64},{96,80},{112,96},{128,112},... | collective-permute-start | bytes 1966088 | tf_op jit(solution)/shard_map/ppermute | solution.py:393
  21.9 1.3 %collective-permute-start.3 = (bf16[2,1024,128]{2,1,0:T(8,128)(2,1)S(1)}, bf16[2,1024,128]{2,1,0:T(8,128)(2,1)S(1)}, u32[]{:S(2)}, u32[]{:S(2)}) collective-permute-start(bf16[2,1024,128]{2,1,0:T(8,128)(2,1)S(1)} %get-tuple-element.18), channel_id=1, source_target_pairs={{16,0},{32,16},{48,32},{64,48},{80,64},{96,80},{112,96},{128,112},... | collective-permute-start | bytes 1572872 | tf_op jit(solution)/shard_map/ppermute | solution.py:393
  23.4 1.3 %collective-permute-start.2 = (bf16[2,512,128]{2,1,0:T(8,128)(2,1)S(1)}, bf16[2,512,128]{2,1,0:T(8,128)(2,1)S(1)}, u32[]{:S(2)}, u32[]{:S(2)}) collective-permute-start(bf16[2,512,128]{2,1,0:T(8,128)(2,1)S(1)} %shard_map.79), channel_id=1, source_target_pairs={{16,0},{32,16},{48,32},{64,48},{80,64},{96,80},{112,96},{128,112},... | collective-permute-start | bytes 786440 | tf_op jit(solution)/shard_map/ppermute | solution.py:393
  24.7 3.5 %shard_map.82.here = f32[384,1152]{1,0:T(8,128)S(1)} custom-call(bf16[4,384,128]{2,1,0:T(8,128)(2,1)S(1)} %collective-permute-done.above.refs_0_, bf16[4,1024,128]{2,1,0:T(8,128)(2,1)S(1)} %get-tuple-element.15.own.up, bf16[4,384,128]{2,1,0:T(8,128)(2,1)S(1)} %collective-permute-done.1.below.refs_1_, bf16[4,1024,128]{2,1,0:T(8,128)(2,1)S(1)} %get-tuple-element.17.saved.s2), custom_call_target="tpu_custom_call" | custom-call | tf_op jit(solution)/shard_map/pallas_call | solution.py:28
  28.3 21.3 %collective-permute-done.3.rest_1_.later = bf16[2,1024,128]{2,1,0:T(8,128)(2,1)S(1)} collective-permute-done((bf16[2,1024,128]{2,1,0:T(8,128)(2,1)S(1)}, bf16[2,1024,128]{2,1,0:T(8,128)(2,1)S(1)}, u32[]{:S(2)}, u32[]{:S(2)}) %collective-permute-start.3) | collective-permute-done | bytes 524320 | tf_op jit(solution)/shard_map/ppermute | solution.py:393
  49.5 2.8 %collective-permute-done.2.rest_0_.edges = bf16[2,512,128]{2,1,0:T(8,128)(2,1)S(1)} collective-permute-done((bf16[2,512,128]{2,1,0:T(8,128)(2,1)S(1)}, bf16[2,512,128]{2,1,0:T(8,128)(2,1)S(1)}, u32[]{:S(2)}, u32[]{:S(2)}) %collective-permute-start.2) | collective-permute-done | bytes 262176 | tf_op jit(solution)/shard_map/ppermute | solution.py:393
  52.3 4.5 %shard_map.80.high = bf16[2,1280,128]{2,1,0:T(8,128)(2,1)S(1)} custom-call(bf16[4,384,128]{2,1,0:T(8,128)(2,1)S(1)} %collective-permute-done.above.refs_0_, bf16[4,1024,128]{2,1,0:T(8,128)(2,1)S(1)} %get-tuple-element.15.own.up, bf16[4,384,128]{2,1,0:T(8,128)(2,1)S(1)} %collective-permute-done.1.below.refs_1_, ...), custom_call_target="tpu_custom_call" | custom-call | tf_op jit(solution)/shard_map/pallas_call | solution.py:28
  56.8 4.8 %shard_map.83 = (bf16[16,216,128]{2,1,0:T(8,128)(2,1)S(1)}, f32[384,1152]{1,0:T(8,128)S(1)}) custom-call(f32[384,1152]{1,0:T(8,128)S(1)} %shard_map.82.here, bf16[2,512,128]{2,1,0:T(8,128)(2,1)S(1)} %collective-permute-done.2.rest_0_.edges, bf16[2,1024,128]{2,1,0:T(8,128)(2,1)S(1)} %collective-permute-done.3.rest_1_.later, ...), custom_call_target="tpu_custom_call" | custom-call | tf_op jit(solution)/shard_map/pallas_call | solution.py:28
  61.6 1.6 %shard_map.84 = (bf16[16,216,128]{2,1,0:T(8,128)(2,1)S(1)}, bf16[16,216,128]{2,1,0:T(8,128)(2,1)S(1)}) custom-call(f32[384,1152]{1,0:T(8,128)S(1)} %get-tuple-element.19.partial, bf16[2,1280,128]{2,1,0:T(8,128)(2,1)S(1)} %collective-permute-done.4.later, bf16[4,1024,128]{2,1,0:T(8,128)(2,1)S(1)} %bitcast.5, bf16[16,216,128]{2,1,0:T(8,128)(2,1)S(1)} %get-tuple-element.20.second), custom_call_target="tpu_custom_call" | custom-call | tf_op jit(solution)/shard_map/pallas_call | solution.py:28
  63.3 2.4 %collective-permute-done.5.other = bf16[16,216,128]{2,1,0:T(8,128)(2,1)S(1)} collective-permute-done((bf16[16,216,128]{2,1,0:T(8,128)(2,1)S(1)}, bf16[16,216,128]{2,1,0:T(8,128)(2,1)S(1)}, u32[]{:S(2)}, u32[]{:S(2)}) %collective-permute-start.5) | collective-permute-done | bytes 884768 | tf_op jit(solution)/shard_map/ppermute | solution.py:445
  65.9 26.6 %all_to_all.15.pieces = bf16[16,216,128]{2,1,0:T(8,128)(2,1)} all-to-all(bf16[16,216,128]{2,1,0:T(8,128)(2,1)S(1)} %shard_map.85), channel_id=1, replica_groups=mesh['z'=8,'yh'=2,'yl'=2,'x'=4,'core'=2] {'yh','yl','x'}, dimensions={0} | all-to-all | bytes 1769472 | tf_op jit(solution)/shard_map/all_to_all | solution.py:397
  92.5 1.3 %shard_map.86 = bf16[8,4,8,128]{3,2,1,0:T(8,128)(2,1)S(1)} custom-call(bf16[16,216,128]{2,1,0:T(8,128)(2,1)} %all_to_all.15.pieces), custom_call_target="tpu_custom_call" | custom-call | tf_op jit(solution)/shard_map/pallas_call | solution.py:28
  93.8 15.3 %all_to_all.16.pieces = bf16[8,4,8,128]{3,2,1,0:T(8,128)(2,1)S(1)} all-to-all(bf16[8,4,8,128]{3,2,1,0:T(8,128)(2,1)S(1)} %shard_map.86), channel_id=1, replica_groups=mesh['z'=8,'yh'=2,'yl'=2,'x'=4,'core'=2] {'z'}, dimensions={0} | all-to-all | bytes 131072 | tf_op jit(solution)/shard_map/all_to_all | solution.py:397
  109.1 0.7 shard_map.87
  109.9 6.2 %all-to-all-start.2 = ((f32[16,4,8,128]{3,2,1,0:T(8,128)}), f32[16,4,8,128]{3,2,1,0:T(8,128)S(1)}, u32[]{:S(2)}, u32[]{:S(2)}) async-start(f32[16,4,8,128]{3,2,1,0:T(8,128)} %shard_map.87), calls=%async_computation.2 | async-start | bytes 524288 | tf_op jit(solution)/shard_map/all_to_all | solution.py:397
  116.0 1.2 copy-done.2
  117.2 6.4 %shard_map.81 = bf16[4,1024,128]{2,1,0:T(8,128)(2,1)} custom-call(bf16[2,1280,128]{2,1,0:T(8,128)(2,1)S(1)} %shard_map.78.low, bf16[2,1280,128]{2,1,0:T(8,128)(2,1)S(1)} %shard_map.80.high, bf16[2,1280,128]{2,1,0:T(8,128)(2,1)S(1)} %collective-permute-done.4.later, bf16[4,1024,128]{2,1,0:T(8,128)(2,1)S(1)} %bitcast.6, bf16[3456,128]{1,0:T(8,128)(2,1)S(1)} %copy-done.2), custom_call_target="tpu_custom_call" | custom-call | tf_op jit(solution)/shard_map/pallas_call | solution.py:28
  123.6 0.7 shard_map.88
  (11 shorter events, 0.9 us)
Async XLA Ops:
  0.6 8.6 %copy-start.1 = (bf16[3456,128]{1,0:T(8,128)(2,1)S(1)}, bf16[3456,128]{1,0:T(8,128)(2,1)}, u32[]{:S(2)}) copy-start(bf16[3456,128]{1,0:T(8,128)(2,1)} %weight.2) | copy-start | bytes 2654212
  2.7 9.2 %collective-permute-start = (bf16[4,384,128]{2,1,0:T(8,128)(2,1)S(1)}, bf16[4,384,128]{2,1,0:T(8,128)(2,1)S(1)}, u32[]{:S(2)}, u32[]{:S(2)}) collective-permute-start(bf16[4,384,128]{2,1,0:T(8,128)(2,1)S(1)} %get-tuple-element.14), channel_id=1, source_target_pairs={{0,1},{1,2},{2,3},{3,4},{4,5},{5,6},{6,7},{7,8},{8,9},{9,10},{10,1... | collective-permute-start | bytes 1179656 | tf_op jit(solution)/shard_map/ppermute | solution.py:393
  7.3 9.1 %collective-permute-start.1 = (bf16[4,384,128]{2,1,0:T(8,128)(2,1)S(1)}, bf16[4,384,128]{2,1,0:T(8,128)(2,1)S(1)}, u32[]{:S(2)}, u32[]{:S(2)}) collective-permute-start(bf16[4,384,128]{2,1,0:T(8,128)(2,1)S(1)} %get-tuple-element.16), channel_id=1, source_target_pairs={{1,0},{2,1},{3,2},{4,3},{5,4},{6,5},{7,6},{8,7},{9,8},{10,9},{11,1... | collective-permute-start | bytes 1179656 | tf_op jit(solution)/shard_map/ppermute | solution.py:393
  20.6 41.0 %collective-permute-start.4 = (bf16[2,1280,128]{2,1,0:T(8,128)(2,1)S(1)}, bf16[2,1280,128]{2,1,0:T(8,128)(2,1)S(1)}, u32[]{:S(2)}, u32[]{:S(2)}) collective-permute-start(bf16[2,1280,128]{2,1,0:T(8,128)(2,1)S(1)} %shard_map.78.low), channel_id=1, source_target_pairs={{16,0},{32,16},{48,32},{64,48},{80,64},{96,80},{112,96},{128,112},... | collective-permute-start | bytes 1966088 | tf_op jit(solution)/shard_map/ppermute | solution.py:393
  21.9 27.6 %collective-permute-start.3 = (bf16[2,1024,128]{2,1,0:T(8,128)(2,1)S(1)}, bf16[2,1024,128]{2,1,0:T(8,128)(2,1)S(1)}, u32[]{:S(2)}, u32[]{:S(2)}) collective-permute-start(bf16[2,1024,128]{2,1,0:T(8,128)(2,1)S(1)} %get-tuple-element.18), channel_id=1, source_target_pairs={{16,0},{32,16},{48,32},{64,48},{80,64},{96,80},{112,96},{128,112},... | collective-permute-start | bytes 1572872 | tf_op jit(solution)/shard_map/ppermute | solution.py:393
  23.4 28.9 %collective-permute-start.2 = (bf16[2,512,128]{2,1,0:T(8,128)(2,1)S(1)}, bf16[2,512,128]{2,1,0:T(8,128)(2,1)S(1)}, u32[]{:S(2)}, u32[]{:S(2)}) collective-permute-start(bf16[2,512,128]{2,1,0:T(8,128)(2,1)S(1)} %shard_map.79), channel_id=1, source_target_pairs={{16,0},{32,16},{48,32},{64,48},{80,64},{96,80},{112,96},{128,112},... | collective-permute-start | bytes 786440 | tf_op jit(solution)/shard_map/ppermute | solution.py:393
  28.3 28.6 %copy-start = (bf16[4,8,128,128]{3,2,1,0:T(8,128)(2,1)S(1)}, bf16[4,8,128,128]{3,2,1,0:T(8,128)(2,1)}, u32[]{:S(2)}) copy-start(bf16[4,8,128,128]{3,2,1,0:T(8,128)(2,1)} %param.6) | copy-start | bytes 3145732
  63.2 2.5 %collective-permute-start.5 = (bf16[16,216,128]{2,1,0:T(8,128)(2,1)S(1)}, bf16[16,216,128]{2,1,0:T(8,128)(2,1)S(1)}, u32[]{:S(2)}, u32[]{:S(2)}) collective-permute-start(bf16[16,216,128]{2,1,0:T(8,128)(2,1)S(1)} %get-tuple-element.22), channel_id=1, source_target_pairs={{0,1},{1,0},{2,3},{3,2},{4,5},{5,4},{6,7},{7,6},{8,9},{9,8},{10,11... | collective-permute-start | bytes 2654216 | tf_op jit(solution)/shard_map/ppermute | solution.py:445
  109.9 13.7 %all-to-all-start.2 = ((f32[16,4,8,128]{3,2,1,0:T(8,128)}), f32[16,4,8,128]{3,2,1,0:T(8,128)S(1)}, u32[]{:S(2)}, u32[]{:S(2)}) async-start(f32[16,4,8,128]{3,2,1,0:T(8,128)} %shard_map.87), calls=%async_computation.2 | async-start | bytes 524288 | tf_op jit(solution)/shard_map/all_to_all | solution.py:397
  116.0 1.2 copy-start.2
